TPU v7x, 512 devices: a whole 4x4x16 slice. The times are simulated.
512 devices in a mesh: dp: 16 (over z_hi, y, core), expert: 32 (over x, z_lo).
Axes of the slice: x: 4, y: 4, z: 16 (z_hi: 2, z_lo: 8; z = z_hi * 8 + z_lo), core: 2. Of those that a mesh axis runs over, the one named last changes fastest.
Arguments:
- tokens: bfloat16 [65536, 1024], P(('dp', 'expert')), may hold values from -6 to 6
- chosen_expert_index: int32 [65536, 6], P(('dp', 'expert')), may hold values from 0 to 31, as said below
- router_gate_weight: float32 [65536, 6], P(('dp', 'expert')), may hold values from 0.05 to 0.5
- output_gradient: bfloat16 [65536, 1024], P(('dp', 'expert')), may hold values from -0.15917969 to 0.15917969
- gate_weight_matrix: bfloat16 [32, 1024, 704], P('expert'), may hold values from -0.1875 to 0.1875
- up_weight: bfloat16 [32, 1024, 704], P('expert'), may hold values from -0.1875 to 0.1875
- down_weight: bfloat16 [32, 704, 1024], P('expert'), may hold values from -0.21875 to 0.21875
- adapter_down_maps: bfloat16 [32, 16, 704], P('expert'), may hold values from -0.21875 to 0.21875
- adapter_up_maps: bfloat16 [32, 16, 1024], P('expert'), may hold values from -1.5 to 1.5
Outputs:
- mixed: bfloat16 [65536, 1024], P(('dp', 'expert'))
- grad_in: bfloat16 [32, 16, 704], P('expert')
- grad_out: bfloat16 [32, 16, 1024], P('expert')
Inputs may be any that keep to these rules, and one draw needn't show every extreme that they name: `chosen_expert_index`: each row names 6 different experts. In each aligned block of 128 rows (the rows of one device) no expert is named by more than 48 rows, and one and the same expert, drawn for the whole array, is named by exactly 48 rows of every block. Each row's experts are 6 neighbours in one circular order of all experts, drawn for the whole array.
All inputs are finite; a program needn't handle non-finite values.
Results may differ from a plain program's by a relative error of at most 0.0064.
Values may be sent and summed in bfloat16 or wider, within the bound.
A program may use at most 64 MiB of HBM per device.

v0:
```python
import jax
import jax.numpy as jnp
from jax import lax
from jax.sharding import PartitionSpec as P


def gathered_total(x, axis):
    pieces = lax.all_gather(x, axis)
    return pieces.sum(axis=0)


def shards(
    tokens,
    chosen_expert_index,
    router_gate_weight,
    output_gradient,
    gate_weight_matrix,
    up_weight,
    down_weight,
    adapter_down_maps,
    adapter_up_maps,
):
    tok_rows, model_width = tokens.shape
    top_count = chosen_expert_index.shape[1]
    adapter_depth = adapter_down_maps.shape[1]
    hidden_width = gate_weight_matrix.shape[2]
    held_experts = gate_weight_matrix.shape[0]
    experts = lax.axis_size("expert") * held_experts
    most_hot = min(2 * tok_rows // experts, tok_rows // top_count)
    slot_cap = top_count * most_hot
    total_slots = tok_rows * top_count
    flat_ids = chosen_expert_index.reshape(total_slots)
    onehot = (flat_ids[:, None] == jnp.arange(experts, dtype=jnp.int32)[None, :]).astype(jnp.int32)
    slot_rank = jnp.sum((jnp.cumsum(onehot, axis=0) - onehot) * onehot, axis=1)
    slot_place = flat_ids * slot_cap + slot_rank
    source_slot = (
        jnp.full((experts * slot_cap,), -1, jnp.int32)
        .at[slot_place]
        .set(jnp.arange(total_slots, dtype=jnp.int32))
    )
    filled = source_slot >= 0
    safe_slot = jnp.maximum(source_slot, 0)
    source_token = safe_slot // top_count
    send_rows = jnp.where(filled[:, None], tokens[source_token], jnp.zeros((), tokens.dtype))
    send_rows = send_rows.reshape(experts, slot_cap, model_width)
    buffer_gates = jnp.where(
        filled, router_gate_weight.reshape(total_slots)[safe_slot], jnp.float32(0.0)
    )
    grad_rows = (buffer_gates[:, None] * output_gradient[source_token].astype(jnp.float32)).astype(
        jnp.bfloat16
    )
    grad_rows = grad_rows.reshape(experts, slot_cap, model_width)
    slot_rows = lax.all_to_all(send_rows, "expert", split_axis=0, concat_axis=0, tiled=True)
    source_count = slot_rows.shape[0]
    item_count = slot_rows.shape[1]
    flat_rows = slot_rows.reshape(source_count * item_count, model_width)
    gate_proj = jnp.dot(flat_rows, gate_weight_matrix[0], preferred_element_type=jnp.float32)
    upward = jnp.dot(flat_rows, up_weight[0], preferred_element_type=jnp.float32)
    hidden_state = (jax.nn.silu(gate_proj) * upward).astype(jnp.bfloat16)
    rank_state = jnp.dot(
        hidden_state, adapter_down_maps[0].T, preferred_element_type=jnp.float32
    ).astype(jnp.bfloat16)
    output = (
        jnp.dot(hidden_state, down_weight[0], preferred_element_type=jnp.float32)
        + jnp.dot(rank_state, adapter_up_maps[0], preferred_element_type=jnp.float32)
    ).astype(jnp.bfloat16)
    output, rank_state, hidden_state = (
        output.reshape(source_count, item_count, model_width),
        rank_state.reshape(source_count, item_count, adapter_depth),
        hidden_state.reshape(source_count, item_count, hidden_width),
    )
    returned = lax.all_to_all(output, "expert", split_axis=0, concat_axis=0, tiled=True)
    slot_out = returned.reshape(experts * slot_cap, model_width)[slot_place].astype(jnp.float32)
    mixed = jnp.sum(
        slot_out.reshape(tok_rows, top_count, model_width) * router_gate_weight[:, :, None], axis=1
    )
    mixed = mixed.astype(jnp.bfloat16)
    recv_grads = lax.all_to_all(grad_rows, "expert", split_axis=0, concat_axis=0, tiled=True)
    flattened_gradient = recv_grads.reshape(-1, model_width)
    received_rank_gradient = jnp.dot(
        flattened_gradient, adapter_up_maps[0].T, preferred_element_type=jnp.float32
    ).astype(jnp.bfloat16)
    grad_model = jnp.dot(
        rank_state.reshape(-1, adapter_depth).T,
        flattened_gradient,
        preferred_element_type=jnp.float32,
    )
    grad_hidden = jnp.dot(
        received_rank_gradient.T,
        hidden_state.reshape(-1, hidden_width),
        preferred_element_type=jnp.float32,
    )
    summed_hidden, summed_model = (
        gathered_total(grad_hidden, "dp"),
        gathered_total(grad_model, "dp"),
    )
    return (
        mixed,
        summed_hidden.astype(jnp.bfloat16)[None],
        summed_model.astype(jnp.bfloat16)[None],
    )


def solution(mesh):
    return jax.shard_map(
        shards,
        mesh=mesh,
        in_specs=(
            P(("dp", "expert"), None),
            P(("dp", "expert"), None),
            P(("dp", "expert"), None),
            P(("dp", "expert"), None),
            P("expert", None, None),
            P("expert", None, None),
            P("expert", None, None),
            P("expert", None, None),
            P("expert", None, None),
        ),
        out_specs=(P(("dp", "expert"), None), P("expert", None, None), P("expert", None, None)),
        check_vma=False,
    )
```

profile of v0, /device:TPU:67, one launch (start us, length us, event | category | flops | bytes accessed | tf_op | source)
XLA Modules:
  0.0 548.7 jit_solution(16783129918749978560)
XLA Ops:
  7.2 0.9 copy.14
  8.1 0.1 eq.29
  8.4 0.7 broadcast_multiply_fusion
  9.1 1.7 reduce-window.6
  10.8 0.3 slice_reduce_fusion
  11.2 0.1 mul.47
  11.5 3.4 scatter_custom_fusion
  14.9 0.8 copy.17
  15.7 0.1 reshape.110
  15.9 5.9 %gather_fusion.2 = f32[1536]{0:T(1024)S(1)} fusion(f32[768]{0:T(1024)S(1)} %reshape.110, s32[2048]{0:T(1024)S(1)} %get-tuple-element.7), kind=kCustom, calls=%fused_computation.2 | custom fusion | bytes 18432 | tf_op jit(solution)/shard_map/gather | solution.py:47
  21.9 5.8 %gather_fusion = bf16[1536,1024]{1,0:T(8,128)(2,1)} fusion(bf16[128,1024]{1,0:T(8,128)(2,1)S(1)} %copy-done.1, s32[2048]{0:T(1024)S(1)} %get-tuple-element.8), kind=kCustom, calls=%fused_computation | custom fusion | bytes 6297600 | tf_op jit(solution)/shard_map/gather | solution.py:44
  27.7 3.3 broadcast_select_fusion
  31.0 14.4 %all-to-all-start = ((bf16[32,48,1024]{2,1,0:T(8,128)(2,1)}), bf16[32,48,1024]{2,1,0:T(8,128)(2,1)}, u32[]{:S(2)}, u32[]{:S(2)}) async-start(bf16[32,48,1024]{2,1,0:T(8,128)(2,1)} %broadcast_select_fusion), calls=%async_computation | async-start | bytes 6291456 | tf_op jit(solution)/shard_map/all_to_all | solution.py:53
  45.4 5.8 %gather_fusion.3 = bf16[1536,1024]{1,0:T(8,128)(2,1)} fusion(bf16[128,1024]{1,0:T(8,128)(2,1)S(1)} %copy-done.2, s32[2048]{0:T(1024)S(1)} %get-tuple-element.8), kind=kCustom, calls=%fused_computation.3 | custom fusion | bytes 6297600 | tf_op jit(solution)/shard_map/gather | solution.py:49
  51.3 4.2 fusion
  55.4 119.8 %all-to-all-done = bf16[32,48,1024]{2,1,0:T(8,128)(2,1)} async-done(((bf16[32,48,1024]{2,1,0:T(8,128)(2,1)}), bf16[32,48,1024]{2,1,0:T(8,128)(2,1)}, u32[]{:S(2)}, u32[]{:S(2)}) %all-to-all-start) | async-done | bytes 3145760 | tf_op jit(solution)/shard_map/all_to_all | solution.py:53
  175.2 18.4 %all-to-all-start.2 = ((bf16[32,48,1024]{2,1,0:T(8,128)(2,1)}), bf16[32,48,1024]{2,1,0:T(8,128)(2,1)}, u32[]{:S(2)}, u32[]{:S(2)}) async-start(bf16[32,48,1024]{2,1,0:T(8,128)(2,1)} %fusion), calls=%async_computation.2 | async-start | bytes 6291456 | tf_op jit(solution)/shard_map/all_to_all | solution.py:78
  193.6 4.9 fusion.4
  198.5 4.6 multiply_convert_fusion
  203.1 0.4 convolution_convert_fusion.1
  203.5 2.7 fusion.1
  206.2 2.7 add_convert_fusion
  208.9 114.5 %all-to-all-done.2 = bf16[32,48,1024]{2,1,0:T(8,128)(2,1)} async-done(((bf16[32,48,1024]{2,1,0:T(8,128)(2,1)}), bf16[32,48,1024]{2,1,0:T(8,128)(2,1)}, u32[]{:S(2)}, u32[]{:S(2)}) %all-to-all-start.2) | async-done | bytes 3145760 | tf_op jit(solution)/shard_map/all_to_all | solution.py:78
  323.4 18.5 %all-to-all-start.1 = ((bf16[32,48,1024]{2,1,0:T(8,128)(2,1)}), bf16[32,48,1024]{2,1,0:T(8,128)(2,1)}, u32[]{:S(2)}, u32[]{:S(2)}) async-start(bf16[32,48,1024]{2,1,0:T(8,128)(2,1)} %bitcast.62), calls=%async_computation.1 | async-start | bytes 6291456 | tf_op jit(solution)/shard_map/all_to_all | solution.py:72
  342.0 3.0 fusion.19
  345.1 4.9 fusion.6
  349.9 176.8 %all-gather = f32[256,704]{1,0:T(8,128)S(1)} all-gather(f32[16,704]{1,0:T(8,128)S(1)} %fusion.6), channel_id=2, replica_groups=mesh['dp'=16,'expert'=32] {'dp'}, dimensions={0}, use_global_device_ids=true | all-gather | bytes 765952 | tf_op jit(solution)/shard_map/all_gather | solution.py:8
  526.7 0.7 reduce_sum.41
  527.4 1.9 reduce_sum.42
  529.3 6.1 %gather_fusion.1 = bf16[768,1024]{1,0:T(8,128)(2,1)S(1)} fusion(bf16[1536,1024]{1,0:T(8,128)(2,1)} %bitcast.9, s32[1024]{0:T(1024)S(1)} %pad_clamp_fusion.2), kind=kCustom, calls=%fused_computation.1 | custom fusion | bytes 3148800 | tf_op jit(solution)/shard_map/gather | solution.py:73
  535.4 2.1 reshape.112
  537.6 4.3 multiply_reduce_fusion
  (31 shorter events, 0.7 us)
Async XLA Ops:
  7.2 196.3 %copy-start = (bf16[1,704,1024]{2,1,0:T(8,128)(2,1)S(1)}, bf16[1,704,1024]{2,1,0:T(8,128)(2,1)}, u32[]{:S(2)}) copy-start(bf16[1,704,1024]{2,1,0:T(8,128)(2,1)} %param.15) | copy-start | bytes 4325380
  15.9 6.0 %copy-start.1 = (bf16[128,1024]{1,0:T(8,128)(2,1)S(1)}, bf16[128,1024]{1,0:T(8,128)(2,1)}, u32[]{:S(2)}) copy-start(bf16[128,1024]{1,0:T(8,128)(2,1)} %param.9) | copy-start | bytes 786436
  31.0 14.5 %copy-start.2 = (bf16[128,1024]{1,0:T(8,128)(2,1)S(1)}, bf16[128,1024]{1,0:T(8,128)(2,1)}, u32[]{:S(2)}) copy-start(bf16[128,1024]{1,0:T(8,128)(2,1)} %param.12) | copy-start | bytes 786436
  31.0 144.2 %all-to-all-start = ((bf16[32,48,1024]{2,1,0:T(8,128)(2,1)}), bf16[32,48,1024]{2,1,0:T(8,128)(2,1)}, u32[]{:S(2)}, u32[]{:S(2)}) async-start(bf16[32,48,1024]{2,1,0:T(8,128)(2,1)} %broadcast_select_fusion), calls=%async_computation | async-start | bytes 6291456 | tf_op jit(solution)/shard_map/all_to_all | solution.py:53
  175.2 148.2 %all-to-all-start.2 = ((bf16[32,48,1024]{2,1,0:T(8,128)(2,1)}), bf16[32,48,1024]{2,1,0:T(8,128)(2,1)}, u32[]{:S(2)}, u32[]{:S(2)}) async-start(bf16[32,48,1024]{2,1,0:T(8,128)(2,1)} %fusion), calls=%async_computation.2 | async-start | bytes 6291456 | tf_op jit(solution)/shard_map/all_to_all | solution.py:78
  193.6 4.9 copy-start.6
  198.5 4.6 copy-start.5
  203.1 3.1 copy-start.3
  203.5 2.7 copy-start.4
  323.4 205.9 %all-to-all-start.1 = ((bf16[32,48,1024]{2,1,0:T(8,128)(2,1)}), bf16[32,48,1024]{2,1,0:T(8,128)(2,1)}, u32[]{:S(2)}, u32[]{:S(2)}) async-start(bf16[32,48,1024]{2,1,0:T(8,128)(2,1)} %bitcast.62), calls=%async_computation.1 | async-start | bytes 6291456 | tf_op jit(solution)/shard_map/all_to_all | solution.py:72
  341.9 185.4 %all-gather.4.cloned.1.call-start = ((), (), s32[]{:S(2)}) async-start(), calls=%async_computation.3 | async-start | bytes 1114112 | tf_op jit(solution)/shard_map/all_gather | solution.py:8
Sparse Core Ops, SparseCore 0:
  346.6 97.2 all-gather.3
where the time goes:
time: 549 us
  waiting for transfers between devices  234 us (43%)
  blocking collectives  177 us (32%)
  starting transfers between devices  51.3 us (9%)
  local copies, waits for them, and re-layouts  32 us (6%)
  matrix products  23.1 us (4%)
  other arithmetic  16.9 us (3%)
  between operations  14.3 us (3%)
    all_gather x1, blocking collectives, gathered_total(): pieces = lax.all_gather(x, axis)  177 us
    all_to_all x1, waiting for transfers between devices, shards(): lax.all_to_all(send_rows, 'expert', split_axis=0, concat_axis=0, tiled=True)  120 us
    all_to_all x1, waiting for transfers between devices, shards(): lax.all_to_all(grad_rows, 'expert', split_axis=0, concat_axis=0, tiled=True)  115 us
    all_to_all x1, starting transfers between devices, shards(): lax.all_to_all(output, 'expert', split_axis=0, concat_axis=0, tiled=True)  18.5 us
    all_to_all x1, starting transfers between devices, shards(): lax.all_to_all(grad_rows, 'expert', split_axis=0, concat_axis=0, tiled=True)  18.4 us
    all_to_all x1, starting transfers between devices, shards(): lax.all_to_all(send_rows, 'expert', split_axis=0, concat_axis=0, tiled=True)  14.4 us
  transfers between devices with their start and end apart: 4, of which 2 were waited for; matrix products, arithmetic and copies ran while one was open for 7% of the time, Pallas kernels for 0%

commit v1 on v0

v1 whole, which is shorter than its diff:
```python
import functools

import jax
import jax.numpy as jnp
from jax import lax
from jax.experimental import pallas as pl
from jax.experimental.pallas import tpu as pltpu
from jax.sharding import PartitionSpec as P

BF = jnp.bfloat16
F32 = jnp.float32
XS, ZL, ZS, YS = 4, 8, 16, 4
CAP = 48
ROWS = XS * CAP
VOID = -1000.0


def mm(a, b):
    return jnp.dot(a, b, preferred_element_type=F32)


def mm_nt(a, b):
    return lax.dot_general(a, b, (((1,), (1,)), ((), ())), preferred_element_type=F32)


def kernel(
    m_ref, tok_hbm, dy_hbm, wg_hbm, wu_hbm, wd_hbm, ad_hbm, au_hbm,
    mixed_ref, gin_ref, gout_ref,
    tbuf, dbuf, mbuf, abuf, wg, wu, wd, ad,
    ssend, srecv, hbuf, osend, oret, lgs, lgr, lrs, lrr, rss, rsr,
    gi, go, gor, dpa, dpr, dpb, dpq, dpo, dpf,
    ld_sem, t_s, t_r, m_s, m_r, d_s, d_r, a_s, a_r, x_s, x_r, lg_s, lg_r,
    o_s, o_r, lr_s, lr_r, r_s, r_r, go_s, go_r, da_s, da_r, db_s, db_r, dc_s, dc_r,
):
    depth = ad_hbm.shape[1]
    hidden = wg_hbm.shape[2]
    toks = tok_hbm.shape[0]
    half = toks // 2
    d = lax.axis_index("dp")
    e = lax.axis_index("expert")
    core = lax.rem(d, 2)
    y = lax.rem(lax.div(d, 2), YS)
    zh = lax.div(d, 2 * YS)
    x = lax.div(e, ZL)
    zl = lax.rem(e, ZL)
    z = zh * ZL + zl
    way = 1 - 2 * core
    k = y * 2 + core

    def at(x_, z_):
        return {"dp": lax.div(z_, ZL) * (2 * YS) + k, "expert": x_ * ZL + lax.rem(z_, ZL)}

    def ring(step):
        return lax.rem(z + step + ZS, ZS)

    def xq(q):
        return lax.rem(x + q + XS, XS)

    def peer(r):
        kk = lax.rem(k + r, 2 * YS)
        return kk, {"dp": zh * (2 * YS) + kk, "expert": e}

    def remote(src, dst, s, r, dev):
        return pltpu.make_async_remote_copy(
            src_ref=src, dst_ref=dst, send_sem=s, recv_sem=r,
            device_id=dev, device_id_type=pl.DeviceIdType.MESH)

    def out_step(i):
        return way * (2 * lax.rem(i, 2) - 1)

    def tok_copy(i, h):
        src = jnp.maximum(i - 2, 0)
        rows = pl.ds(h * half, half)
        return remote(tbuf.at[src, rows], tbuf.at[i, rows], t_s.at[i, h], t_r.at[i, h],
                      at(x, ring(out_step(i))))

    def dy_copy(i):
        src = jnp.maximum(i - 2, 0)
        return remote(dbuf.at[src], dbuf.at[i], d_s.at[i], d_r.at[i], at(x, ring(out_step(i))))

    def m_copy(i):
        zt = ring(out_step(i) * ((i + 1) // 2))
        return remote(m_ref.at[lax.rem(zt, ZL)], mbuf.at[i], m_s.at[i], m_r.at[i], at(x, zt))

    def a_copy(q):
        return remote(abuf.at[pl.ds(0, depth)], abuf.at[pl.ds(q * depth, depth)],
                      a_s.at[q], a_r.at[q], at(xq(-q), z))

    def x_copy(i, q):
        rows = pl.ds(q * CAP, CAP)
        return remote(ssend.at[i, rows], srecv.at[i, rows], x_s.at[i, q], x_r.at[i, q], at(xq(q), z))

    def lg_copy(i, q):
        rows = pl.ds(q * depth, depth)
        return remote(lgs.at[i, rows], lgr.at[i, rows], lg_s.at[i, q], lg_r.at[i, q], at(xq(q), z))

    def o_copy(i, q):
        rows = pl.ds(q * CAP, CAP)
        return remote(osend.at[i, rows], oret.at[i, rows], o_s.at[i, q], o_r.at[i, q], at(xq(-q), z))

    def lr_copy(i, q):
        rows = pl.ds(q * depth, depth)
        return remote(lrs.at[i, rows], lrr.at[i, rows], lr_s.at[i, q], lr_r.at[i, q], at(xq(-q), z))

    def rs_copy(i):
        return remote(rss.at[i], rsr.at[i], r_s.at[i], r_r.at[i], at(x, ring(-out_step(i))))

    def go_copy(q):
        return remote(go.at[pl.ds(q * depth, depth)], gor.at[pl.ds(q * depth, depth)],
                      go_s.at[q], go_r.at[q], at(xq(q), z))

    def da_copy(r):
        kk, dev = peer(r)
        return remote(dpa.at[kk], dpr.at[r], da_s.at[r], da_r.at[r], dev)

    def db_copy():
        return remote(dpb, dpq, db_s, db_r, at(x, ring(ZL)))

    def dc_copy(r):
        _, dev = peer(r)
        return remote(dpo, dpf.at[r], dc_s.at[r], dc_r.at[r], dev)

    loads = [
        pltpu.make_async_copy(tok_hbm, tbuf.at[0], ld_sem.at[0]),
        pltpu.make_async_copy(au_hbm.at[0], abuf.at[pl.ds(0, depth)], ld_sem.at[1]),
        pltpu.make_async_copy(wg_hbm.at[0], wg, ld_sem.at[2]),
        pltpu.make_async_copy(wu_hbm.at[0], wu, ld_sem.at[3]),
        pltpu.make_async_copy(wd_hbm.at[0], wd, ld_sem.at[4]),
        pltpu.make_async_copy(ad_hbm.at[0], ad, ld_sem.at[5]),
        pltpu.make_async_copy(dy_hbm, dbuf.at[0], ld_sem.at[6]),
    ]
    for load in loads:
        load.start()

    barrier = pltpu.get_barrier_semaphore()
    friends = [at(x, ring(s)) for s in (1, -1, 2, -2, 3, -3, 4, -4, ZL)]
    friends += [at(xq(q), z) for q in range(1, XS)]
    friends += [peer(r)[1] for r in range(1, 2 * YS)]
    for friend in friends:
        pl.semaphore_signal(barrier, inc=1, device_id=friend, device_id_type=pl.DeviceIdType.MESH)
    gi[...] = jnp.zeros_like(gi)
    go[...] = jnp.zeros_like(go)
    mbuf[0] = m_ref[zl]
    loads[0].wait()
    loads[1].wait()
    pl.semaphore_wait(barrier, len(friends))

    for i in (1, 2):
        for h in (0, 1):
            tok_copy(i, h).start()
    for i in range(1, 8):
        m_copy(i).start()
    for q in range(1, XS):
        a_copy(q).start()

    row_id = lax.broadcasted_iota(jnp.int32, (CAP, toks), 0).astype(F32)
    row_all = lax.broadcasted_iota(jnp.int32, (toks, toks), 0).astype(F32)
    lane_id = lax.broadcasted_iota(jnp.int32, (toks, ROWS), 1).astype(F32)

    def compact(i):
        m = mbuf[i]
        hot = jnp.concatenate(
            [(row_id == m[XS + q:XS + q + 1]).astype(F32) for q in range(XS)], axis=0).astype(BF)
        rows = mm(hot, tbuf[i]).astype(BF)
        srecv[i, 0:CAP] = rows[0:CAP]
        ssend[i, CAP:ROWS] = rows[CAP:ROWS]
        for q in range(1, XS):
            x_copy(i, q).start()

    def expert(i):
        for q in range(1, XS):
            x_copy(i, q).wait_recv()
        rows = srecv[i]
        g = mm(rows, wg[...])
        u = mm(rows, wu[...])
        h = (g / (1.0 + jnp.exp(-g)) * u).astype(BF)
        hbuf[i] = h
        adm = ad[...]
        low = mm_nt(h, adm).astype(BF)
        for q in range(XS):
            t = mm_nt(adm, h[q * CAP:(q + 1) * CAP]).astype(BF)
            if q == 0:
                lrr[i, 0:depth, 0:CAP] = t
            else:
                lrs[i, q * depth:(q + 1) * depth, 0:CAP] = t
        out = (mm(h, wd[...]) + mm(low, abuf[0:depth])).astype(BF)
        oret[i, 0:CAP] = out[0:CAP]
        osend[i, CAP:ROWS] = out[CAP:ROWS]
        for q in range(1, XS):
            lr_copy(i, q).start()

    compact(0)
    for load in loads[2:]:
        load.wait()

    def inbound(i, c):
        for h in (0, 1):
            tok_copy(i, h).wait_recv()

        @pl.when(i <= 5)
        def _():
            for h in (0, 1):
                tok_copy(i + 2, h).start()

        @pl.when(i == 6)
        def _():
            dy_copy(1).start()
            dy_copy(2).start()

        m_copy_wait(i)
        compact(i)
        expert(i - 1)
        return c

    def m_copy_wait(i):
        remote(m_ref.at[0], mbuf.at[i], m_s.at[i], m_r.at[i], at(x, z)).wait_recv()

    lax.fori_loop(1, 8, inbound, 0)
    for q in range(1, XS):
        a_copy(q).wait_recv()
    for q in range(1, XS):
        o_copy(6, q).start()
    expert(7)
    for q in range(1, XS):
        o_copy(7, q).start()

    def grad_in(n):
        for q in range(1, XS):
            lg_copy(n, q).wait_recv()
        acc = gi[:, 0:hidden]
        for q in range(XS):
            acc += mm(lgr[n, q * depth:(q + 1) * depth, 0:CAP], hbuf[n, q * CAP:(q + 1) * CAP])
        gi[:, 0:hidden] = acc

    def outbound(n, c):
        i = 7 - n

        @pl.when(i >= 2)
        def _():
            for q in range(1, XS):
                o_copy(i - 2, q).start()

        for q in range(1, XS):
            o_copy(i, q).wait_recv()
        mt = mbuf[i].T
        wt = jnp.zeros((toks, ROWS), F32)
        for q in range(XS):
            wt = jnp.where(lane_id == mt[:, XS + q:XS + q + 1] + float(q * CAP), mt[:, q:q + 1], wt)
        hi = wt.astype(BF)
        lo = (wt - hi.astype(F32)).astype(BF)
        rows = oret[i]
        part = mm(hi, rows) + mm(lo, rows)

        @pl.when(i >= 6)
        def _():
            rss[i] = part.astype(BF)

        @pl.when((i >= 1) & (i < 6))
        def _():
            rs_copy(i + 2).wait_recv()
            rss[i] = (part + rsr[i + 2].astype(F32)).astype(BF)

        @pl.when(i >= 1)
        def _():
            rs_copy(i).start()

        @pl.when(i == 0)
        def _():
            rs_copy(1).wait_recv()
            rs_copy(2).wait_recv()
            mixed_ref[...] = (part + rsr[1].astype(F32) + rsr[2].astype(F32)).astype(BF)

        @pl.when(n >= 1)
        def _():
            dy_copy(n).wait_recv()

        @pl.when((n >= 1) & (n <= 5))
        def _():
            dy_copy(n + 2).start()

        m = mbuf[n]
        dy = dbuf[n]
        base = mm_nt(abuf[...], dy)
        lows = []
        for q in range(XS):
            gate = m[q:q + 1]
            rank = m[XS + q:XS + q + 1]
            lg = (base[q * depth:(q + 1) * depth] * gate).astype(BF)
            hot = (row_all == rank).astype(F32).astype(BF)
            packed = mm_nt(lg, hot).astype(BF)
            if q == 0:
                lgr[n, 0:depth] = packed
            else:
                lgs[n, q * depth:(q + 1) * depth] = packed
                lg_copy(n, q).start()
                lr_copy(n, q).wait_recv()
            low = mm(lrr[n, q * depth:(q + 1) * depth, 0:CAP], hot[0:CAP])
            lows.append((low * gate).astype(BF))
        go[...] += mm(jnp.concatenate(lows, axis=0), dy)

        @pl.when(n >= 1)
        def _():
            grad_in(n - 1)

        return c

    lax.fori_loop(0, 8, outbound, 0)

    for q in range(1, XS):
        go_copy(q).start()
    grad_in(7)
    total = go[0:depth]
    for q in range(1, XS):
        go_copy(q).wait_recv()
        total += gor[q * depth:(q + 1) * depth]
    for j in range(2 * YS):
        cols = slice(j * 128, (j + 1) * 128)
        dpa[j, 0:depth] = total[:, cols]
        if j * 128 < hidden:
            dpa[j, depth:2 * depth] = gi[:, cols]
        else:
            dpa[j, depth:2 * depth] = jnp.zeros((depth, 128), F32)
    for r in range(1, 2 * YS):
        da_copy(r).start()
    own = dpa[k]
    for r in range(1, 2 * YS):
        da_copy(r).wait_recv()
        own += dpr[r]
    dpb[...] = own
    db_copy().start()
    db_copy().wait_recv()
    fin = (dpb[...] + dpq[...]).astype(BF)
    dpo[...] = fin
    dpf[0] = fin
    for r in range(1, 2 * YS):
        dc_copy(r).start()
    for r in range(1, 2 * YS):
        dc_copy(r).wait_recv()
    for j in range(2 * YS):
        piece = dpf[lax.rem(k - j + 2 * YS, 2 * YS)]
        gout_ref[:, j * 128:(j + 1) * 128] = piece[0:depth]
        width = min(128, hidden - j * 128)
        if width > 0:
            gin_ref[:, j * 128:j * 128 + width] = piece[depth:2 * depth, 0:width]

    def drain(i, c):
        for q in range(1, XS):
            x_copy(i, q).wait_send()
            lg_copy(i, q).wait_send()
            o_copy(i, q).wait_send()
            lr_copy(i, q).wait_send()

        @pl.when(i >= 1)
        def _():
            for h in (0, 1):
                tok_copy(i, h).wait_send()
            dy_copy(i).wait_send()
            remote(m_ref.at[0], mbuf.at[i], m_s.at[i], m_r.at[i], at(x, z)).wait_send()
            rs_copy(i).wait_send()
            da_copy(i).wait_send()
            dc_copy(i).wait_send()

        return c

    lax.fori_loop(0, 8, drain, 0)
    db_copy().wait_send()
    for q in range(1, XS):
        a_copy(q).wait_send()
        go_copy(q).wait_send()


def shards(tokens, ids, gates, dy, wg, wu, wd, ad, au):
    toks, width = tokens.shape
    depth, hidden = ad.shape[1], ad.shape[2]
    x = lax.axis_index("expert") // ZL
    table = ((x + jnp.arange(XS)[None, :]) % XS) * ZL + jnp.arange(ZL)[:, None]
    hit = ids.T[:, None, None, :] == table.astype(jnp.int32)[None, :, :, None]
    gate = jnp.sum(jnp.where(hit, gates.T[:, None, None, :], 0.0), axis=0)
    chosen = jnp.any(hit, axis=0)
    before = jnp.arange(toks)[:, None] < jnp.arange(toks)[None, :]
    rank = jnp.dot(chosen.astype(BF).reshape(XS * ZL, toks), before.astype(BF),
                   preferred_element_type=F32).reshape(ZL, XS, toks)
    m = jnp.concatenate([gate, jnp.where(chosen, rank, VOID)], axis=1)
    anyspace = pl.BlockSpec(memory_space=pl.ANY)
    vmem = pl.BlockSpec(memory_space=pltpu.VMEM)
    dma = pltpu.SemaphoreType.DMA
    V = pltpu.VMEM
    mixed, gin, gout = pl.pallas_call(
        kernel,
        name="moe",
        out_shape=(
            jax.ShapeDtypeStruct((toks, width), BF),
            jax.ShapeDtypeStruct((depth, hidden), BF),
            jax.ShapeDtypeStruct((depth, width), BF),
        ),
        in_specs=[vmem] + [anyspace] * 7,
        out_specs=(vmem, vmem, vmem),
        scratch_shapes=[
            V((8, toks, width), BF), V((8, toks, width), BF), V((8, 2 * XS, toks), F32),
            V((XS * depth, width), BF),
            V((width, hidden), BF), V((width, hidden), BF), V((hidden, width), BF), V((depth, hidden), BF),
            V((8, ROWS, width), BF), V((8, ROWS, width), BF), V((8, ROWS, hidden), BF),
            V((8, ROWS, width), BF), V((8, ROWS, width), BF),
            V((8, XS * depth, 128), BF), V((8, XS * depth, 128), BF),
            V((8, XS * depth, 128), BF), V((8, XS * depth, 128), BF),
            V((8, toks, width), BF), V((8, toks, width), BF),
            V((depth, 768), F32), V((XS * depth, width), F32), V((XS * depth, width), F32),
            V((8, 2 * depth, 128), F32), V((8, 2 * depth, 128), F32),
            V((2 * depth, 128), F32), V((2 * depth, 128), F32), V((2 * depth, 128), BF),
            V((8, 2 * depth, 128), BF),
            dma((7,)), dma((8, 2)), dma((8, 2)), dma((8,)), dma((8,)), dma((8,)), dma((8,)),
            dma((4,)), dma((4,)), dma((8, 4)), dma((8, 4)), dma((8, 4)), dma((8, 4)),
            dma((8, 4)), dma((8, 4)), dma((8, 4)), dma((8, 4)), dma((8,)), dma((8,)),
            dma((4,)), dma((4,)), dma((8,)), dma((8,)), dma(()), dma(()), dma((8,)), dma((8,)),
        ],
        compiler_params=pltpu.CompilerParams(
            collective_id=0, has_side_effects=True, vmem_limit_bytes=60 * 1024 * 1024),
    )(m, tokens, dy, wg, wu, wd, ad, au)
    return mixed, gin[None], gout[None]


def solution(mesh):
    tok = P(("dp", "expert"), None)
    exp = P("expert", None, None)
    return jax.shard_map(
        shards,
        mesh=mesh,
        in_specs=(tok, tok, tok, tok, exp, exp, exp, exp, exp),
        out_specs=(tok, exp, exp),
        check_vma=False,
    )
```

time: 549 us -> 141 us (0.26)
  the two profiles are of different devices: /device:TPU:67 before, /device:TPU:1 now
where the time goes in v1:
time: 141 us
  Pallas kernels  129 us (91%)
  local copies, waits for them, and re-layouts  8.66 us (6%)
  other arithmetic  2.27 us (2%)
    pallas_call x1, Pallas kernels, shards(): pl.pallas_call(kernel, name='moe', out_shape=(jax.ShapeDtypeStruct((toks,...  129 us
    unnamed x7, local copies, waits for them, and re-layouts  8.65 us

profile of v1, /device:TPU:1, one launch (start us, length us, event | category | flops | bytes accessed | tf_op | source)
XLA Modules:
  0.0 140.9 jit_solution(16775972371023728198)
XLA Ops:
  0.7 0.1 iota_add_fusion
  0.7 0.8 compare_reduce_fusion
  1.5 0.1 convolution_select_fusion
  1.6 0.8 fusion
  2.4 0.6 pad_maximum_fusion.m_ref
  3.1 0.0 copy-start
  3.1 2.7 %copy.19.wg_hbm = bf16[1,1024,704]{2,1,0:T(8,128)(2,1)} copy(bf16[1,1024,704]{1,2,0:T(8,128)(2,1)} %param.13) | data formatting | bytes 2883584 | tf_op args[4]
  5.8 0.0 copy-done
  5.8 1.6 %copy.20.wu_hbm = bf16[1,1024,704]{2,1,0:T(8,128)(2,1)} copy(bf16[1,1024,704]{1,2,0:T(8,128)(2,1)S(1)} %copy-done) | data formatting | bytes 2883584 | tf_op args[5]
  7.3 129.2 %moe.1 = (bf16[128,1024]{1,0:T(8,128)(2,1)}, bf16[16,704]{1,0:T(8,128)(2,1)}, bf16[16,1024]{1,0:T(8,128)(2,1)}) custom-call(f32[8,8,128]{2,1,0:T(8,128)} %pad_maximum_fusion.m_ref, bf16[128,1024]{1,0:T(8,128)(2,1)} %tok_hbm.1, bf16[128,1024]{1,0:T(8,128)(2,1)} %dy_hbm.1, bf16[1,1024,704]{2,1,0:T(8,128)(2,1)} %copy.19.wg_hbm, ...), custom_call_target="tpu_custom_call" | custom-call | tf_op jit(solution)/shard_map/moe/pallas_call | solution.py:388
  136.5 1.7 %copy.27 = bf16[128,1024]{1,0:T(8,128)(2,1)} copy(bf16[128,1024]{1,0:T(8,128)(2,1)} %get-tuple-element.12) | data formatting | bytes 524288
  138.2 1.3 copy.28
  139.6 1.4 copy.29
  (2 shorter events, 0.0 us)
Async XLA Ops:
  3.1 2.7 %copy-start = (bf16[1,1024,704]{1,2,0:T(8,128)(2,1)S(1)}, bf16[1,1024,704]{1,2,0:T(8,128)(2,1)}, u32[]{:S(2)}) copy-start(bf16[1,1024,704]{1,2,0:T(8,128)(2,1)} %param.14) | copy-start | bytes 4325380

commit v2 on v1

--- a/solution.py
+++ b/solution.py
@@ -24,16 +24,17 @@
 
 
 def kernel(
-    m_ref, tok_hbm, dy_hbm, wg_hbm, wu_hbm, wd_hbm, ad_hbm, au_hbm,
+    ids_ref, gates_ref, tok_hbm, dy_hbm, wg_hbm, wu_hbm, wd_hbm, ad_hbm, au_hbm,
     mixed_ref, gin_ref, gout_ref,
-    tbuf, dbuf, mbuf, abuf, wg, wu, wd, ad,
+    tbuf, dbuf, m_ref, mbuf, abuf, wg, wu, wd, ad,
     ssend, srecv, hbuf, osend, oret, lgs, lgr, lrs, lrr, rss, rsr,
     gi, go, gor, dpa, dpr, dpb, dpq, dpo, dpf,
     ld_sem, t_s, t_r, m_s, m_r, d_s, d_r, a_s, a_r, x_s, x_r, lg_s, lg_r,
-    o_s, o_r, lr_s, lr_r, r_s, r_r, go_s, go_r, da_s, da_r, db_s, db_r, dc_s, dc_r,
+    o_s, o_r, lr_s, lr_r, r_s, r_r, go_s, go_r, da_s, da_r, db_s, db_r, dc_s, dc_r, far,
 ):
     depth = ad_hbm.shape[1]
-    hidden = wg_hbm.shape[2]
+    hidden = wg_hbm.shape[1]
+    choices = ids_ref.shape[0]
     toks = tok_hbm.shape[0]
     half = toks // 2
     d = lax.axis_index("dp")
@@ -133,25 +134,40 @@
         load.start()
 
     barrier = pltpu.get_barrier_semaphore()
-    friends = [at(x, ring(s)) for s in (1, -1, 2, -2, 3, -3, 4, -4, ZL)]
+    friends = [at(x, ring(s)) for s in (1, -1, 2, -2, 3, -3, 4, -4)]
     friends += [at(xq(q), z) for q in range(1, XS)]
     friends += [peer(r)[1] for r in range(1, 2 * YS)]
     for friend in friends:
         pl.semaphore_signal(barrier, inc=1, device_id=friend, device_id_type=pl.DeviceIdType.MESH)
+
+    ids_t = ids_ref[...].astype(F32)
+    gates_t = gates_ref[...]
+    slot = lax.broadcasted_iota(jnp.int32, (XS * ZL, 1), 0)
+    owner = (lax.rem(x + lax.div(slot, ZL), XS) * ZL + lax.rem(slot, ZL)).astype(F32)
+    gate_all = jnp.zeros((XS * ZL, toks), F32)
+    hits = jnp.zeros((XS * ZL, toks), F32)
+    for c in range(choices):
+        hit = ids_t[c:c + 1] == owner
+        gate_all += jnp.where(hit, gates_t[c:c + 1], 0.0)
+        hits += hit.astype(F32)
+    before = (lax.broadcasted_iota(jnp.int32, (toks, toks), 0)
+              < lax.broadcasted_iota(jnp.int32, (toks, toks), 1)).astype(F32).astype(BF)
+    rank_all = jnp.where(hits > 0.0, mm(hits.astype(BF), before), VOID)
+    for q in range(XS):
+        m_ref[:, q, :] = gate_all[q * ZL:(q + 1) * ZL]
+        m_ref[:, XS + q, :] = rank_all[q * ZL:(q + 1) * ZL]
+    mbuf[0] = m_ref[zl]
     gi[...] = jnp.zeros_like(gi)
     go[...] = jnp.zeros_like(go)
-    mbuf[0] = m_ref[zl]
     loads[0].wait()
-    loads[1].wait()
     pl.semaphore_wait(barrier, len(friends))
 
-    for i in (1, 2):
-        for h in (0, 1):
+    for h in (0, 1):
+        for i in (1, 2):
             tok_copy(i, h).start()
     for i in range(1, 8):
         m_copy(i).start()
-    for q in range(1, XS):
-        a_copy(q).start()
+    pl.semaphore_signal(far, inc=1, device_id=at(x, ring(-4)), device_id_type=pl.DeviceIdType.MESH)
 
     row_id = lax.broadcasted_iota(jnp.int32, (CAP, toks), 0).astype(F32)
     row_all = lax.broadcasted_iota(jnp.int32, (toks, toks), 0).astype(F32)
@@ -171,8 +187,8 @@
         for q in range(1, XS):
             x_copy(i, q).wait_recv()
         rows = srecv[i]
-        g = mm(rows, wg[...])
-        u = mm(rows, wu[...])
+        g = mm_nt(rows, wg[...])
+        u = mm_nt(rows, wu[...])
         h = (g / (1.0 + jnp.exp(-g)) * u).astype(BF)
         hbuf[i] = h
         adm = ad[...]
@@ -189,40 +205,8 @@
         for q in range(1, XS):
             lr_copy(i, q).start()
 
-    compact(0)
-    for load in loads[2:]:
-        load.wait()
-
-    def inbound(i, c):
-        for h in (0, 1):
-            tok_copy(i, h).wait_recv()
-
-        @pl.when(i <= 5)
-        def _():
-            for h in (0, 1):
-                tok_copy(i + 2, h).start()
-
-        @pl.when(i == 6)
-        def _():
-            dy_copy(1).start()
-            dy_copy(2).start()
-
-        m_copy_wait(i)
-        compact(i)
-        expert(i - 1)
-        return c
-
-    def m_copy_wait(i):
+    def m_wait(i):
         remote(m_ref.at[0], mbuf.at[i], m_s.at[i], m_r.at[i], at(x, z)).wait_recv()
-
-    lax.fori_loop(1, 8, inbound, 0)
-    for q in range(1, XS):
-        a_copy(q).wait_recv()
-    for q in range(1, XS):
-        o_copy(6, q).start()
-    expert(7)
-    for q in range(1, XS):
-        o_copy(7, q).start()
 
     def grad_in(n):
         for q in range(1, XS):
@@ -232,52 +216,7 @@
             acc += mm(lgr[n, q * depth:(q + 1) * depth, 0:CAP], hbuf[n, q * CAP:(q + 1) * CAP])
         gi[:, 0:hidden] = acc
 
-    def outbound(n, c):
-        i = 7 - n
-
-        @pl.when(i >= 2)
-        def _():
-            for q in range(1, XS):
-                o_copy(i - 2, q).start()
-
-        for q in range(1, XS):
-            o_copy(i, q).wait_recv()
-        mt = mbuf[i].T
-        wt = jnp.zeros((toks, ROWS), F32)
-        for q in range(XS):
-            wt = jnp.where(lane_id == mt[:, XS + q:XS + q + 1] + float(q * CAP), mt[:, q:q + 1], wt)
-        hi = wt.astype(BF)
-        lo = (wt - hi.astype(F32)).astype(BF)
-        rows = oret[i]
-        part = mm(hi, rows) + mm(lo, rows)
-
-        @pl.when(i >= 6)
-        def _():
-            rss[i] = part.astype(BF)
-
-        @pl.when((i >= 1) & (i < 6))
-        def _():
-            rs_copy(i + 2).wait_recv()
-            rss[i] = (part + rsr[i + 2].astype(F32)).astype(BF)
-
-        @pl.when(i >= 1)
-        def _():
-            rs_copy(i).start()
-
-        @pl.when(i == 0)
-        def _():
-            rs_copy(1).wait_recv()
-            rs_copy(2).wait_recv()
-            mixed_ref[...] = (part + rsr[1].astype(F32) + rsr[2].astype(F32)).astype(BF)
-
-        @pl.when(n >= 1)
-        def _():
-            dy_copy(n).wait_recv()
-
-        @pl.when((n >= 1) & (n <= 5))
-        def _():
-            dy_copy(n + 2).start()
-
+    def grads(n):
         m = mbuf[n]
         dy = dbuf[n]
         base = mm_nt(abuf[...], dy)
@@ -298,42 +237,150 @@
             lows.append((low * gate).astype(BF))
         go[...] += mm(jnp.concatenate(lows, axis=0), dy)
 
-        @pl.when(n >= 1)
-        def _():
-            grad_in(n - 1)
-
-        return c
-
-    lax.fori_loop(0, 8, outbound, 0)
-
+    def dy_in(i):
+        dy_copy(i).wait_recv()
+        if i + 2 <= 7:
+            dy_copy(i + 2).start()
+
+    compact(0)
+    loads[1].wait()
+    for q in range(1, XS):
+        a_copy(q).start()
+    for load in loads[2:]:
+        load.wait()
+
+    for pair in ((1, 2), (3, 4), (5, 6), (7,)):
+        for h in (0, 1):
+            for i in pair:
+                tok_copy(i, h).wait_recv()
+                if i + 2 <= 7:
+                    tok_copy(i + 2, h).start()
+        if pair == (3, 4):
+            dy_copy(2).start()
+        if pair == (5, 6):
+            dy_copy(1).start()
+        for i in pair:
+            m_wait(i)
+            compact(i)
+        if pair == (1, 2):
+            expert(0)
+            for q in range(1, XS):
+                a_copy(q).wait_recv()
+        if pair == (3, 4):
+            expert(1)
+            expert(2)
+            grads(0)
+        if pair == (5, 6):
+            expert(3)
+            expert(4)
+    dy_in(2)
+    expert(5)
+    for q in range(1, XS):
+        o_copy(5, q).start()
+    expert(6)
+    for q in range(1, XS):
+        o_copy(6, q).start()
+    dy_in(1)
+    expert(7)
+    for q in range(1, XS):
+        o_copy(7, q).start()
+
+    def combine(i):
+        for q in range(1, XS):
+            o_copy(i, q).wait_recv()
+        mt = mbuf[i].T
+        wt = jnp.zeros((toks, ROWS), F32)
+        for q in range(XS):
+            wt = jnp.where(lane_id == mt[:, XS + q:XS + q + 1] + float(q * CAP), mt[:, q:q + 1], wt)
+        hi = wt.astype(BF)
+        lo = (wt - hi.astype(F32)).astype(BF)
+        rows = oret[i]
+        part = mm(hi, rows) + mm(lo, rows)
+        if i >= 6:
+            rss[i] = part.astype(BF)
+        elif i >= 1:
+            rs_copy(i + 2).wait_recv()
+            rss[i] = (part + rsr[i + 2].astype(F32)).astype(BF)
+        else:
+            rs_copy(1).wait_recv()
+            rs_copy(2).wait_recv()
+            mixed_ref[...] = (part + rsr[1].astype(F32) + rsr[2].astype(F32)).astype(BF)
+        if i >= 1:
+            rs_copy(i).start()
+
+    def returns(i):
+        for q in range(1, XS):
+            o_copy(i, q).start()
+
+    def sum_a():
+        for q in range(1, XS):
+            go_copy(q).wait_recv()
+        total = go[0:depth] + gor[depth:2 * depth] + gor[2 * depth:3 * depth] + gor[3 * depth:4 * depth]
+        for j in range(2 * YS):
+            cols = slice(j * 128, (j + 1) * 128)
+            dpa[j, 0:depth] = total[:, cols]
+            if j * 128 < hidden:
+                dpa[j, depth:2 * depth] = gi[:, cols]
+            else:
+                dpa[j, depth:2 * depth] = jnp.zeros((depth, 128), F32)
+        for r in range(1, 2 * YS):
+            da_copy(r).start()
+
+    def sum_b():
+        own = dpa[k]
+        for r in range(1, 2 * YS):
+            da_copy(r).wait_recv()
+            own += dpr[r]
+        dpb[...] = own
+        pl.semaphore_wait(far, 1)
+        db_copy().start()
+
+    def sum_c():
+        db_copy().wait_recv()
+        fin = (dpb[...] + dpq[...]).astype(BF)
+        dpo[...] = fin
+        dpf[0] = fin
+        for r in range(1, 2 * YS):
+            dc_copy(r).start()
+
+    combine(7)
+    returns(4)
+    dy_in(4)
+    dy_in(3)
+    grads(2)
+    combine(6)
+    grads(1)
+    returns(3)
+    grads(4)
+    combine(5)
+    dy_in(6)
+    dy_in(5)
+    grads(3)
+    returns(2)
+    grad_in(0)
+    grad_in(2)
+    combine(4)
+    grads(6)
+    returns(1)
+    grad_in(1)
+    grad_in(4)
+    combine(3)
+    dy_in(7)
+    grads(5)
+    grads(7)
     for q in range(1, XS):
         go_copy(q).start()
+    returns(0)
+    grad_in(3)
+    grad_in(6)
+    combine(2)
+    grad_in(5)
+    combine(1)
     grad_in(7)
-    total = go[0:depth]
-    for q in range(1, XS):
-        go_copy(q).wait_recv()
-        total += gor[q * depth:(q + 1) * depth]
-    for j in range(2 * YS):
-        cols = slice(j * 128, (j + 1) * 128)
-        dpa[j, 0:depth] = total[:, cols]
-        if j * 128 < hidden:
-            dpa[j, depth:2 * depth] = gi[:, cols]
-        else:
-            dpa[j, depth:2 * depth] = jnp.zeros((depth, 128), F32)
-    for r in range(1, 2 * YS):
-        da_copy(r).start()
-    own = dpa[k]
-    for r in range(1, 2 * YS):
-        da_copy(r).wait_recv()
-        own += dpr[r]
-    dpb[...] = own
-    db_copy().start()
-    db_copy().wait_recv()
-    fin = (dpb[...] + dpq[...]).astype(BF)
-    dpo[...] = fin
-    dpf[0] = fin
-    for r in range(1, 2 * YS):
-        dc_copy(r).start()
+    sum_a()
+    combine(0)
+    sum_b()
+    sum_c()
     for r in range(1, 2 * YS):
         dc_copy(r).wait_recv()
     for j in range(2 * YS):
@@ -369,18 +416,15 @@
         go_copy(q).wait_send()
 
 
+def settle(a_ref, b_ref, c_ref, ao_ref, bo_ref, co_ref):
+    ao_ref[...] = a_ref[...]
+    bo_ref[0] = b_ref[...]
+    co_ref[0] = c_ref[...]
+
+
 def shards(tokens, ids, gates, dy, wg, wu, wd, ad, au):
     toks, width = tokens.shape
     depth, hidden = ad.shape[1], ad.shape[2]
-    x = lax.axis_index("expert") // ZL
-    table = ((x + jnp.arange(XS)[None, :]) % XS) * ZL + jnp.arange(ZL)[:, None]
-    hit = ids.T[:, None, None, :] == table.astype(jnp.int32)[None, :, :, None]
-    gate = jnp.sum(jnp.where(hit, gates.T[:, None, None, :], 0.0), axis=0)
-    chosen = jnp.any(hit, axis=0)
-    before = jnp.arange(toks)[:, None] < jnp.arange(toks)[None, :]
-    rank = jnp.dot(chosen.astype(BF).reshape(XS * ZL, toks), before.astype(BF),
-                   preferred_element_type=F32).reshape(ZL, XS, toks)
-    m = jnp.concatenate([gate, jnp.where(chosen, rank, VOID)], axis=1)
     anyspace = pl.BlockSpec(memory_space=pl.ANY)
     vmem = pl.BlockSpec(memory_space=pltpu.VMEM)
     dma = pltpu.SemaphoreType.DMA
@@ -393,12 +437,12 @@
             jax.ShapeDtypeStruct((depth, hidden), BF),
             jax.ShapeDtypeStruct((depth, width), BF),
         ),
-        in_specs=[vmem] + [anyspace] * 7,
+        in_specs=[vmem, vmem] + [anyspace] * 7,
         out_specs=(vmem, vmem, vmem),
         scratch_shapes=[
-            V((8, toks, width), BF), V((8, toks, width), BF), V((8, 2 * XS, toks), F32),
+            V((8, toks, width), BF), V((8, toks, width), BF), V((ZL, 2 * XS, toks), F32), V((8, 2 * XS, toks), F32),
             V((XS * depth, width), BF),
-            V((width, hidden), BF), V((width, hidden), BF), V((hidden, width), BF), V((depth, hidden), BF),
+            V((hidden, width), BF), V((hidden, width), BF), V((hidden, width), BF), V((depth, hidden), BF),
             V((8, ROWS, width), BF), V((8, ROWS, width), BF), V((8, ROWS, hidden), BF),
             V((8, ROWS, width), BF), V((8, ROWS, width), BF),
             V((8, XS * depth, 128), BF), V((8, XS * depth, 128), BF),
@@ -412,11 +456,23 @@
             dma((4,)), dma((4,)), dma((8, 4)), dma((8, 4)), dma((8, 4)), dma((8, 4)),
             dma((8, 4)), dma((8, 4)), dma((8, 4)), dma((8, 4)), dma((8,)), dma((8,)),
             dma((4,)), dma((4,)), dma((8,)), dma((8,)), dma(()), dma(()), dma((8,)), dma((8,)),
+            pltpu.SemaphoreType.REGULAR,
         ],
         compiler_params=pltpu.CompilerParams(
-            collective_id=0, has_side_effects=True, vmem_limit_bytes=60 * 1024 * 1024),
-    )(m, tokens, dy, wg, wu, wd, ad, au)
-    return mixed, gin[None], gout[None]
+            collective_id=0, has_side_effects=True, vmem_limit_bytes=61 * 1024 * 1024),
+    )(ids.T, gates.T, tokens, dy, wg.swapaxes(1, 2), wu.swapaxes(1, 2), wd, ad, au)
+    mixed, gin, gout = pl.pallas_call(
+        settle,
+        name="settle",
+        out_shape=(
+            jax.ShapeDtypeStruct((toks, width), BF),
+            jax.ShapeDtypeStruct((1, depth, hidden), BF),
+            jax.ShapeDtypeStruct((1, depth, width), BF),
+        ),
+        in_specs=[vmem] * 3,
+        out_specs=(vmem, vmem, vmem),
+    )(mixed, gin, gout)
+    return mixed, gin, gout
 
 
 def solution(mesh):

time: 141 us -> 121 us (0.86)
  Pallas kernels: 129 us -> 120 us
  local copies, waits for them, and re-layouts: 8.66 us -> 0 us
  other arithmetic: 2.27 us -> 0 us
    pallas_call x1, Pallas kernels: 129 us -> 118 us  [shards(): pl.pallas_call(kernel, name='moe', out_shape=(jax.ShapeDtypeStruct((toks,...]
    unnamed x7 -> x0, local copies, waits for them, and re-layouts: 8.65 us -> none
    pallas_call x0 -> x1, Pallas kernels: none -> 1.7 us  [shards(): pl.pallas_call(settle, name='settle', out_shape=(jax.ShapeDtypeStruct((to...]
where the time goes in v2:
time: 121 us
  Pallas kernels  120 us (99%)
    pallas_call x1, Pallas kernels, shards(): pl.pallas_call(kernel, name='moe', out_shape=(jax.ShapeDtypeStruct((toks,...  118 us

profile of v2, /device:TPU:1, one launch (start us, length us, event | category | flops | bytes accessed | tf_op | source)
XLA Modules:
  0.0 120.6 jit_solution(12955966817132955949)
XLA Ops:
  0.6 118.3 %moe.1 = (bf16[128,1024]{1,0:T(8,128)(2,1)}, bf16[16,704]{1,0:T(8,128)(2,1)}, bf16[16,1024]{1,0:T(8,128)(2,1)}) custom-call(s32[6,128]{1,0:T(8,128)} %bitcast.6, f32[6,128]{1,0:T(8,128)} %bitcast.7, bf16[128,1024]{1,0:T(8,128)(2,1)} %tok_hbm.1, bf16[128,1024]{1,0:T(8,128)(2,1)} %dy_hbm.1, bf16[1,704,1024]{2,1,0:T(8,128)(2,1)} %bitcast.4, ...), custom_call_target="tpu_custom_call" | custom-call | tf_op jit(solution)/shard_map/moe/pallas_call | solution.py:432
  118.9 1.7 %settle.1 = (bf16[128,1024]{1,0:T(8,128)(2,1)}, bf16[1,16,704]{2,1,0:T(8,128)(2,1)}, bf16[1,16,1024]{2,1,0:T(8,128)(2,1)}) custom-call(bf16[128,1024]{1,0:T(8,128)(2,1)} %get-tuple-element.6.a_ref, bf16[16,704]{1,0:T(8,128)(2,1)} %get-tuple-element.7.b_ref, bf16[16,1024]{1,0:T(8,128)(2,1)} %get-tuple-element.8.c_ref), custom_call_target="tpu_custom_call" | custom-call | tf_op jit(solution)/shard_map/settle/pallas_call | solution.py:464

commit v3 on v2

v3 whole, which is shorter than its diff:
```python
import functools

import jax
import jax.numpy as jnp
from jax import lax
from jax.experimental import pallas as pl
from jax.experimental.pallas import tpu as pltpu
from jax.sharding import PartitionSpec as P

BF = jnp.bfloat16
F32 = jnp.float32
XS, ZL, ZS, YS = 4, 8, 16, 4
CAP = 48
ROWS = XS * CAP
VOID = -1000.0


def mm(a, b):
    return jnp.dot(a, b, preferred_element_type=F32)


def mm_nt(a, b):
    return lax.dot_general(a, b, (((1,), (1,)), ((), ())), preferred_element_type=F32)


def kernel(
    ids_hbm, gates_hbm, tok_hbm, dy_hbm, wg_hbm, wu_hbm, wd_hbm, ad_hbm, au_hbm,
    mixed_ref, gin_ref, gout_ref,
    tbuf, dbuf, own, idg, mbuf, abuf, wg, wu, wd, ad,
    ssend, srecv, hbuf, osend, oret, lgs, lgr, lrs, lrr, rss, rsr,
    gi, go, gob, gor, dpa, dpr, dpb, dpq, dpo, dpf,
    ld_sem, t_s, t_r, m_s, m_r, d_s, d_r, a_s, a_r, x_s, x_r, lg_s, lg_r,
    o_s, o_r, lr_s, lr_r, r_s, r_r, go_s, go_r, da_s, da_r, db_s, db_r, dc_s, dc_r, far,
):
    depth = ad_hbm.shape[1]
    hidden = wg_hbm.shape[1]
    choices = ids_hbm.shape[0]
    toks = tok_hbm.shape[0]
    half = toks // 2
    d = lax.axis_index("dp")
    e = lax.axis_index("expert")
    core = lax.rem(d, 2)
    y = lax.rem(lax.div(d, 2), YS)
    zh = lax.div(d, 2 * YS)
    x = lax.div(e, ZL)
    zl = lax.rem(e, ZL)
    z = zh * ZL + zl
    way = 1 - 2 * core
    k = y * 2 + core

    def at(x_, z_):
        return {"dp": lax.div(z_, ZL) * (2 * YS) + k, "expert": x_ * ZL + lax.rem(z_, ZL)}

    def ring(step):
        return lax.rem(z + step + ZS, ZS)

    def xq(q):
        return lax.rem(x + q + XS, XS)

    def peer(r):
        kk = lax.rem(k + r, 2 * YS)
        return kk, {"dp": zh * (2 * YS) + kk, "expert": e}

    def remote(src, dst, s, r, dev):
        return pltpu.make_async_remote_copy(
            src_ref=src, dst_ref=dst, send_sem=s, recv_sem=r,
            device_id=dev, device_id_type=pl.DeviceIdType.MESH)

    def group(ref, s):
        return remote(ref, ref, s, s, at(x, z))

    def three(ref, i, size):
        return ref.at[i, pl.ds(size, 3 * size)]

    def out_step(i):
        return way * (2 * lax.rem(i, 2) - 1)

    def tok_copy(i, h):
        src = jnp.maximum(i - 2, 0)
        rows = pl.ds(h * half, half)
        return remote(tbuf.at[src, rows], tbuf.at[i, rows], t_s.at[jnp.minimum(i, 2) - 1], t_r.at[i, h],
                      at(x, ring(out_step(i))))

    def dy_copy(i):
        src = jnp.maximum(i - 2, 0)
        return remote(dbuf.at[src], dbuf.at[i], d_s, d_r.at[i], at(x, ring(out_step(i))))

    def m_copy(i):
        src = jnp.maximum(i - 2, 0)
        return remote(idg.at[src], idg.at[i], m_s, m_r.at[i], at(x, ring(out_step(i))))

    def a_copy(q):
        return remote(abuf.at[pl.ds(0, depth)], abuf.at[pl.ds(q * depth, depth)],
                      a_s, a_r, at(xq(-q), z))

    def x_copy(i, q):
        rows = pl.ds(q * CAP, CAP)
        return remote(ssend.at[i, rows], srecv.at[i, rows], x_s, x_r.at[i], at(xq(q), z))

    def lg_copy(i, q):
        rows = pl.ds(q * depth, depth)
        return remote(lgs.at[i, rows], lgr.at[i, rows], lg_s, lg_r.at[i], at(xq(q), z))

    def o_copy(i, q):
        rows = pl.ds(q * CAP, CAP)
        return remote(osend.at[i, rows], oret.at[i, rows], o_s, o_r.at[i], at(xq(-q), z))

    def lr_copy(i, q):
        rows = pl.ds(q * depth, depth)
        return remote(lrs.at[i, rows], lrr.at[i, rows], lr_s, lr_r.at[i], at(xq(-q), z))

    def rs_copy(i, h):
        rows = pl.ds(h * half, half)
        return remote(rss.at[i, rows], rsr.at[i, rows], r_s, r_r.at[i, h],
                      at(x, ring(-out_step(i))))

    def go_copy(q):
        return remote(gob.at[pl.ds(q * depth, depth)], gor.at[pl.ds(q * depth, depth)],
                      go_s, go_r, at(xq(q), z))

    def da_copy(r):
        kk, dev = peer(r)
        return remote(dpa.at[kk], dpr.at[r], da_s, da_r, dev)

    def db_copy():
        return remote(dpb, dpq, db_s, db_r, at(x, ring(ZL)))

    def dc_copy(r):
        _, dev = peer(r)
        return remote(dpo, dpf.at[r], dc_s, dc_r, dev)

    loads = [
        pltpu.make_async_copy(tok_hbm, tbuf.at[0], ld_sem.at[0]),
        pltpu.make_async_copy(au_hbm.at[0], abuf.at[pl.ds(0, depth)], ld_sem.at[1]),
        pltpu.make_async_copy(wg_hbm.at[0], wg, ld_sem.at[2]),
        pltpu.make_async_copy(wu_hbm.at[0], wu, ld_sem.at[3]),
        pltpu.make_async_copy(wd_hbm.at[0], wd, ld_sem.at[4]),
        pltpu.make_async_copy(ad_hbm.at[0], ad, ld_sem.at[5]),
        pltpu.make_async_copy(dy_hbm, dbuf.at[0], ld_sem.at[6]),
        pltpu.make_async_copy(ids_hbm, own, ld_sem.at[7]),
        pltpu.make_async_copy(gates_hbm, idg.at[0, pl.ds(0, choices)], ld_sem.at[8]),
    ]
    barrier = pltpu.get_barrier_semaphore()
    friends = [at(x, ring(s)) for s in (1, -1)]
    friends += [at(xq(q), z) for q in range(1, XS)]
    friends += [peer(r)[1] for r in range(1, 2 * YS)]
    for friend in friends:
        pl.semaphore_signal(barrier, inc=1, device_id=friend, device_id_type=pl.DeviceIdType.MESH)
    for j in (0, 8, 7, 1, 6, 2, 3, 4, 5):
        loads[j].start()

    slot = lax.broadcasted_iota(jnp.int32, (XS, 1), 0)
    owner = (lax.rem(x + slot, XS) * ZL + zl).astype(F32)
    before = (lax.broadcasted_iota(jnp.int32, (toks, toks), 0)
              < lax.broadcasted_iota(jnp.int32, (toks, toks), 1)).astype(F32).astype(BF)
    gi[...] = jnp.zeros_like(gi)
    go[...] = jnp.zeros_like(go)
    loads[7].wait()
    loads[8].wait()
    idg[0, 8:8 + choices] = own[...].astype(F32)
    loads[0].wait()
    pl.semaphore_wait(barrier, len(friends))

    m_copy(1).start()
    for h in (0, 1):
        tok_copy(1, h).start()

    row_id = lax.broadcasted_iota(jnp.int32, (CAP, toks), 0).astype(F32)
    row_all = lax.broadcasted_iota(jnp.int32, (toks, toks), 0).astype(F32)
    lane_id = lax.broadcasted_iota(jnp.int32, (toks, ROWS), 1).astype(F32)

    def route(i):
        gate = jnp.zeros((XS, toks), F32)
        hits = jnp.zeros((XS, toks), F32)
        for c in range(choices):
            hit = idg[i, 8 + c:9 + c] == owner
            gate += jnp.where(hit, idg[i, c:c + 1], 0.0)
            hits += hit.astype(F32)
        m = jnp.concatenate([gate, jnp.where(hits > 0.0, mm(hits.astype(BF), before), VOID)], axis=0)
        mbuf[i] = m
        return m

    def compact(i):
        m = route(i)
        hot = jnp.concatenate(
            [(row_id == m[XS + q:XS + q + 1]).astype(F32) for q in range(XS)], axis=0).astype(BF)
        rows = mm(hot, tbuf[i]).astype(BF)
        srecv[i, 0:CAP] = rows[0:CAP]
        ssend[i, CAP:ROWS] = rows[CAP:ROWS]
        for q in range(1, XS):
            x_copy(i, q).start()

    def expert(i):
        group(three(srecv, i, CAP), x_r.at[i]).wait_recv()
        rows = srecv[i]
        g = mm_nt(rows, wg[...])
        u = mm_nt(rows, wu[...])
        h = (g / (1.0 + jnp.exp(-g)) * u).astype(BF)
        hbuf[i] = h
        adm = ad[...]
        low = mm_nt(h, adm).astype(BF)
        for q in range(XS):
            t = mm_nt(adm, h[q * CAP:(q + 1) * CAP]).astype(BF)
            if q == 0:
                lrr[i, 0:depth, 0:CAP] = t
            else:
                lrs[i, q * depth:(q + 1) * depth, 0:CAP] = t
        out = (mm(h, wd[...]) + mm(low, abuf[0:depth])).astype(BF)
        oret[i, 0:CAP] = out[0:CAP]
        osend[i, CAP:ROWS] = out[CAP:ROWS]
        for q in range(1, XS):
            lr_copy(i, q).start()

    def grad_in(n):
        group(three(lgr, n, depth), lg_r.at[n]).wait_recv()
        acc = gi[:, 0:hidden]
        for q in range(XS):
            acc += mm(lgr[n, q * depth:(q + 1) * depth, 0:CAP], hbuf[n, q * CAP:(q + 1) * CAP])
        gi[:, 0:hidden] = acc

    def grads(n):
        m = mbuf[n]
        dy = dbuf[n]
        base = mm_nt(abuf[...], dy)
        lows = []
        for q in range(XS):
            gate = m[q:q + 1]
            rank = m[XS + q:XS + q + 1]
            lg = (base[q * depth:(q + 1) * depth] * gate).astype(BF)
            hot = (row_all == rank).astype(F32).astype(BF)
            packed = mm_nt(lg, hot).astype(BF)
            if q == 0:
                lgr[n, 0:depth] = packed
            else:
                lgs[n, q * depth:(q + 1) * depth] = packed
                lg_copy(n, q).start()
            if q == 1:
                group(three(lrr, n, depth), lr_r.at[n]).wait_recv()
            low = mm(lrr[n, q * depth:(q + 1) * depth, 0:CAP], hot[0:CAP])
            lows.append((low * gate).astype(BF))
        go[...] += mm(jnp.concatenate(lows, axis=0), dy)

    def dy_in(i):
        dy_copy(i).wait_recv()
        if i + 2 <= 7:
            dy_copy(i + 2).start()

    def pass_on(i, h):
        if h == 0:
            m_copy(i).start()
        tok_copy(i, h).start()

    def tokens_in(i):
        m_copy(i).wait_recv()
        for h in (0, 1):
            tok_copy(i, h).wait_recv()
            if 1 < i <= 5:
                pass_on(i + 2, h)
        compact(i)
        if i == 1:
            pass_on(3, 0)
            pass_on(3, 1)

    def returns(i):
        for q in range(1, XS):
            o_copy(i, q).start()

    compact(0)
    group(tbuf.at[0], t_s.at[0]).wait_send()
    m_copy(2).start()
    for h in (0, 1):
        tok_copy(2, h).start()
    for j in (1, 6, 2, 3, 4, 5):
        loads[j].wait()
    for q in range(1, XS):
        a_copy(q).start()
    tokens_in(1)
    expert(0)
    tokens_in(2)
    tokens_in(3)
    dy_copy(1).start()
    expert(1)
    tokens_in(4)
    dy_copy(2).start()
    expert(2)
    tokens_in(5)
    expert(3)
    tokens_in(6)
    group(abuf.at[pl.ds(depth, 3 * depth)], a_r).wait_recv()
    grads(0)
    expert(4)
    tokens_in(7)
    pl.semaphore_signal(far, inc=1, device_id=at(x, ring(-4 * way)), device_id_type=pl.DeviceIdType.MESH)
    dy_in(1)
    dy_in(2)
    expert(5)
    grads(1)
    grads(2)
    expert(6)
    returns(6)
    dy_in(4)
    dy_in(3)
    expert(7)
    returns(7)
    returns(5)
    grads(4)
    grad_in(0)
    dy_in(6)
    grads(3)
    dy_in(5)
    grad_in(1)
    grad_in(2)

    def combine(i):
        group(three(oret, i, CAP), o_r.at[i]).wait_recv()
        mt = mbuf[i].T
        wt = jnp.zeros((toks, ROWS), F32)
        for q in range(XS):
            wt = jnp.where(lane_id == mt[:, XS + q:XS + q + 1] + float(q * CAP), mt[:, q:q + 1], wt)
        hi = wt.astype(BF)
        lo = (wt - hi.astype(F32)).astype(BF)
        rows = oret[i]
        for h in (0, 1):
            keep = slice(h * half, (h + 1) * half)
            both = mm(jnp.concatenate([hi[keep], lo[keep]], axis=0), rows)
            part = both[0:half] + both[half:]
            if i == 0:
                for j in (1, 2):
                    rs_copy(j, h).wait_recv()
                    part += rsr[j, keep].astype(F32)
                mixed_ref[keep] = part.astype(BF)
                continue
            if i < 6:
                rs_copy(i + 2, h).wait_recv()
                part += rsr[i + 2, keep].astype(F32)
            rss[i, keep] = part.astype(BF)
            rs_copy(i, h).start()

    def sum_a():
        group(gor.at[pl.ds(depth, 3 * depth)], go_r).wait_recv()
        total = go[0:depth]
        for q in range(1, XS):
            total += gor[q * depth:(q + 1) * depth].astype(F32)
        for j in range(2 * YS):
            cols = slice(j * 128, (j + 1) * 128)
            dpa[j, 0:depth] = total[:, cols]
            if j * 128 < hidden:
                dpa[j, depth:2 * depth] = gi[:, cols]
            else:
                dpa[j, depth:2 * depth] = jnp.zeros((depth, 128), F32)
        for r in range(1, 2 * YS):
            da_copy(r).start()

    def sum_b():
        mine = dpa[k]
        group(dpr.at[pl.ds(1, 2 * YS - 1)], da_r).wait_recv()
        for r in range(1, 2 * YS):
            mine += dpr[r]
        dpb[...] = mine
        pl.semaphore_wait(far, 1)
        db_copy().start()

    def sum_c():
        db_copy().wait_recv()
        fin = (dpb[...] + dpq[...]).astype(BF)
        dpo[...] = fin
        dpf[0] = fin
        for r in range(1, 2 * YS):
            dc_copy(r).start()

    combine(7)
    returns(4)
    grads(6)
    grads(5)
    combine(6)
    dy_in(7)
    grads(7)
    gob[...] = go[...].astype(BF)
    for q in range(1, XS):
        go_copy(q).start()
    returns(3)
    combine(5)
    returns(2)
    grad_in(4)
    grad_in(3)
    grad_in(6)
    grad_in(5)
    grad_in(7)
    sum_a()
    combine(4)
    returns(1)
    combine(3)
    returns(0)
    sum_b()
    combine(2)
    combine(1)
    sum_c()
    combine(0)
    group(dpf.at[pl.ds(1, 2 * YS - 1)], dc_r).wait_recv()
    for j in range(2 * YS):
        piece = dpf[lax.rem(k - j + 2 * YS, 2 * YS)]
        gout_ref[:, j * 128:(j + 1) * 128] = piece[0:depth]
        width = min(128, hidden - j * 128)
        if width > 0:
            gin_ref[:, j * 128:j * 128 + width] = piece[depth:2 * depth, 0:width]

    seven = pl.ds(1, 7)
    group(tbuf.at[pl.ds(2, 6)], t_s.at[1]).wait_send()
    group(idg.at[seven], m_s).wait_send()
    group(dbuf.at[seven], d_s).wait_send()
    group(rss.at[seven], r_s).wait_send()
    group(abuf.at[pl.ds(depth, 3 * depth)], a_s).wait_send()
    group(gob.at[pl.ds(depth, 3 * depth)], go_s).wait_send()
    group(ssend.at[:, pl.ds(CAP, 3 * CAP)], x_s).wait_send()
    group(osend.at[:, pl.ds(CAP, 3 * CAP)], o_s).wait_send()
    group(lgs.at[:, pl.ds(depth, 3 * depth)], lg_s).wait_send()
    group(lrs.at[:, pl.ds(depth, 3 * depth)], lr_s).wait_send()
    group(dpr.at[seven], da_s).wait_send()
    group(dpf.at[seven], dc_s).wait_send()
    db_copy().wait_send()


def settle(a_ref, b_ref, c_ref, ao_ref, bo_ref, co_ref):
    ao_ref[...] = a_ref[...]
    bo_ref[0] = b_ref[...]
    co_ref[0] = c_ref[...]


def shards(tokens, ids, gates, dy, wg, wu, wd, ad, au):
    toks, width = tokens.shape
    depth, hidden = ad.shape[1], ad.shape[2]
    anyspace = pl.BlockSpec(memory_space=pl.ANY)
    vmem = pl.BlockSpec(memory_space=pltpu.VMEM)
    dma = pltpu.SemaphoreType.DMA
    V = pltpu.VMEM
    mixed, gin, gout = pl.pallas_call(
        kernel,
        name="moe",
        out_shape=(
            jax.ShapeDtypeStruct((toks, width), BF),
            jax.ShapeDtypeStruct((depth, hidden), BF),
            jax.ShapeDtypeStruct((depth, width), BF),
        ),
        in_specs=[anyspace] * 9,
        out_specs=(vmem, vmem, vmem),
        scratch_shapes=[
            V((8, toks, width), BF), V((8, toks, width), BF), V(ids.shape[::-1], ids.dtype), V((8, 16, toks), F32),
            V((8, 2 * XS, toks), F32),
            V((XS * depth, width), BF),
            V((hidden, width), BF), V((hidden, width), BF), V((hidden, width), BF), V((depth, hidden), BF),
            V((8, ROWS, width), BF), V((8, ROWS, width), BF), V((8, ROWS, hidden), BF),
            V((8, ROWS, width), BF), V((8, ROWS, width), BF),
            V((8, XS * depth, 128), BF), V((8, XS * depth, 128), BF),
            V((8, XS * depth, 128), BF), V((8, XS * depth, 128), BF),
            V((8, toks, width), BF), V((8, toks, width), BF),
            V((depth, 768), F32), V((XS * depth, width), F32), V((XS * depth, width), BF), V((XS * depth, width), BF),
            V((8, 2 * depth, 128), F32), V((8, 2 * depth, 128), F32),
            V((2 * depth, 128), F32), V((2 * depth, 128), F32), V((2 * depth, 128), BF),
            V((8, 2 * depth, 128), BF),
            dma((9,)), dma((2,)), dma((8, 2)), dma(()), dma((8,)), dma(()), dma((8,)), dma(()), dma(()),
            dma(()), dma((8,)), dma(()), dma((8,)), dma(()), dma((8,)), dma(()), dma((8,)),
            dma(()), dma((8, 2)), dma(()), dma(()), dma(()), dma(()), dma(()), dma(()), dma(()), dma(()),
            pltpu.SemaphoreType.REGULAR,
        ],
        compiler_params=pltpu.CompilerParams(
            collective_id=0, has_side_effects=True, vmem_limit_bytes=61 * 1024 * 1024),
    )(ids.T, gates.T, tokens, dy, wg.swapaxes(1, 2), wu.swapaxes(1, 2), wd, ad, au)
    mixed, gin, gout = pl.pallas_call(
        settle,
        name="settle",
        out_shape=(
            jax.ShapeDtypeStruct((toks, width), BF),
            jax.ShapeDtypeStruct((1, depth, hidden), BF),
            jax.ShapeDtypeStruct((1, depth, width), BF),
        ),
        in_specs=[vmem] * 3,
        out_specs=(vmem, vmem, vmem),
    )(mixed, gin, gout)
    return mixed, gin, gout


def solution(mesh):
    tok = P(("dp", "expert"), None)
    exp = P("expert", None, None)
    return jax.shard_map(
        shards,
        mesh=mesh,
        in_specs=(tok, tok, tok, tok, exp, exp, exp, exp, exp),
        out_specs=(tok, exp, exp),
        check_vma=False,
    )
```

time: 121 us -> 99.7 us (0.82); the launches traced: 121 us -> 97.9 us
  Pallas kernels: 120 us -> 97.2 us
    pallas_call x1, Pallas kernels: 118 us -> 95.5 us  [shards(): pl.pallas_call(kernel, name='moe', out_shape=(jax.ShapeDtypeStruct((toks,...]
where the time goes in v3:
time: 99.7 us; the launch traced here: 97.9 us
  Pallas kernels  97.2 us (97%)
    pallas_call x1, Pallas kernels, shards(): pl.pallas_call(kernel, name='moe', out_shape=(jax.ShapeDtypeStruct((toks,...  95.5 us

profile of v3, /device:TPU:1, one launch (start us, length us, event | category | flops | bytes accessed | tf_op | source)
XLA Modules:
  0.0 97.9 jit_solution(14528181199994887459)
XLA Ops:
  0.6 95.5 %moe.1 = (bf16[128,1024]{1,0:T(8,128)(2,1)}, bf16[16,704]{1,0:T(8,128)(2,1)}, bf16[16,1024]{1,0:T(8,128)(2,1)}) custom-call(s32[6,128]{1,0:T(8,128)} %bitcast.6, f32[6,128]{1,0:T(8,128)} %bitcast.7, bf16[128,1024]{1,0:T(8,128)(2,1)} %tok_hbm.1, bf16[128,1024]{1,0:T(8,128)(2,1)} %dy_hbm.1, bf16[1,704,1024]{2,1,0:T(8,128)(2,1)} %bitcast.4, ...), custom_call_target="tpu_custom_call" | custom-call | tf_op jit(solution)/shard_map/moe/pallas_call | solution.py:436
  96.2 1.7 %settle.1 = (bf16[128,1024]{1,0:T(8,128)(2,1)}, bf16[1,16,704]{2,1,0:T(8,128)(2,1)}, bf16[1,16,1024]{2,1,0:T(8,128)(2,1)}) custom-call(bf16[128,1024]{1,0:T(8,128)(2,1)} %get-tuple-element.6.a_ref, bf16[16,704]{1,0:T(8,128)(2,1)} %get-tuple-element.7.b_ref, bf16[16,1024]{1,0:T(8,128)(2,1)} %get-tuple-element.8.c_ref), custom_call_target="tpu_custom_call" | custom-call | tf_op jit(solution)/shard_map/settle/pallas_call | solution.py:468

commit v4 on v3

--- a/solution.py
+++ b/solution.py
@@ -13,6 +13,8 @@
 CAP = 48
 ROWS = XS * CAP
 VOID = -1000.0
+TILE = (0, 1, 1, 2, 2, 3, 3, 4)
+SIDE = (0, 0, 1, 1, 0, 1, 0, 0)
 
 
 def mm(a, b):
@@ -82,8 +84,9 @@
                       at(x, ring(out_step(i))))
 
     def dy_copy(i):
-        src = jnp.maximum(i - 2, 0)
-        return remote(dbuf.at[src], dbuf.at[i], d_s, d_r.at[i], at(x, ring(out_step(i))))
+        hops = 2 if i == 7 else 1
+        return remote(dbuf.at[max(i - 2 * hops, 0)], dbuf.at[i], d_s, d_r.at[i],
+                      at(x, ring(out_step(i) * hops)))
 
     def m_copy(i):
         src = jnp.maximum(i - 2, 0)
@@ -199,51 +202,72 @@
         hbuf[i] = h
         adm = ad[...]
         low = mm_nt(h, adm).astype(BF)
+        p, lanes = i // 2, slice(i % 2 * CAP, (i % 2 + 1) * CAP)
         for q in range(XS):
             t = mm_nt(adm, h[q * CAP:(q + 1) * CAP]).astype(BF)
             if q == 0:
-                lrr[i, 0:depth, 0:CAP] = t
+                lrr[p, 0:depth, lanes] = t
             else:
-                lrs[i, q * depth:(q + 1) * depth, 0:CAP] = t
+                lrs[p, q * depth:(q + 1) * depth, lanes] = t
         out = (mm(h, wd[...]) + mm(low, abuf[0:depth])).astype(BF)
         oret[i, 0:CAP] = out[0:CAP]
         osend[i, CAP:ROWS] = out[CAP:ROWS]
-        for q in range(1, XS):
-            lr_copy(i, q).start()
-
-    def grad_in(n):
-        group(three(lgr, n, depth), lg_r.at[n]).wait_recv()
+        if i % 2 == 1:
+            for q in range(1, XS):
+                lr_copy(p, q).start()
+
+    def grad_in(t):
+        group(three(lgr, t, depth), lg_r.at[t]).wait_recv()
         acc = gi[:, 0:hidden]
-        for q in range(XS):
-            acc += mm(lgr[n, q * depth:(q + 1) * depth, 0:CAP], hbuf[n, q * CAP:(q + 1) * CAP])
+        for n in range(8):
+            if TILE[n] != t:
+                continue
+            lanes = slice(SIDE[n] * CAP, (SIDE[n] + 1) * CAP)
+            for q in range(XS):
+                acc += mm(lgr[t, q * depth:(q + 1) * depth, lanes], hbuf[n, q * CAP:(q + 1) * CAP])
         gi[:, 0:hidden] = acc
 
+    seen_low = []
+    seen_tile = []
+
     def grads(n):
+        t, p = TILE[n], n // 2
+        rows = slice(SIDE[n] * CAP, (SIDE[n] + 1) * CAP)
+        lanes = slice(n % 2 * CAP, (n % 2 + 1) * CAP)
+        if p not in seen_low:
+            seen_low.append(p)
+            group(three(lrr, p, depth), lr_r.at[p]).wait_recv()
         m = mbuf[n]
         dy = dbuf[n]
         base = mm_nt(abuf[...], dy)
         lows = []
+        packs = []
         for q in range(XS):
             gate = m[q:q + 1]
             rank = m[XS + q:XS + q + 1]
             lg = (base[q * depth:(q + 1) * depth] * gate).astype(BF)
-            hot = (row_all == rank).astype(F32).astype(BF)
-            packed = mm_nt(lg, hot).astype(BF)
-            if q == 0:
-                lgr[n, 0:depth] = packed
-            else:
-                lgs[n, q * depth:(q + 1) * depth] = packed
-                lg_copy(n, q).start()
-            if q == 1:
-                group(three(lrr, n, depth), lr_r.at[n]).wait_recv()
-            low = mm(lrr[n, q * depth:(q + 1) * depth, 0:CAP], hot[0:CAP])
+            hot = (row_all == rank + float(SIDE[n] * CAP)).astype(F32).astype(BF)
+            packs.append(mm_nt(lg, hot))
+            low = mm(lrr[p, q * depth:(q + 1) * depth, lanes], hot[rows])
             lows.append((low * gate).astype(BF))
+        pack = jnp.concatenate(packs, axis=0)
+        if t in seen_tile:
+            pack += lgs[t].astype(F32)
+        lgs[t] = pack.astype(BF)
+        last = t in seen_tile or TILE.count(t) == 1
+        seen_tile.append(t)
+        if last:
+            for q in range(1, XS):
+                lg_copy(t, q).start()
+            lgr[t, 0:depth] = pack[0:depth].astype(BF)
         go[...] += mm(jnp.concatenate(lows, axis=0), dy)
 
     def dy_in(i):
         dy_copy(i).wait_recv()
-        if i + 2 <= 7:
+        if i <= 4:
             dy_copy(i + 2).start()
+        if i == 3:
+            dy_copy(7).start()
 
     def pass_on(i, h):
         if h == 0:
@@ -289,13 +313,13 @@
     group(abuf.at[pl.ds(depth, 3 * depth)], a_r).wait_recv()
     grads(0)
     expert(4)
+    dy_in(2)
+    dy_in(1)
     tokens_in(7)
     pl.semaphore_signal(far, inc=1, device_id=at(x, ring(-4 * way)), device_id_type=pl.DeviceIdType.MESH)
-    dy_in(1)
-    dy_in(2)
-    expert(5)
     grads(1)
     grads(2)
+    expert(5)
     expert(6)
     returns(6)
     dy_in(4)
@@ -304,12 +328,16 @@
     returns(7)
     returns(5)
     grads(4)
-    grad_in(0)
+    grads(3)
     dy_in(6)
-    grads(3)
+    grads(6)
     dy_in(5)
-    grad_in(1)
-    grad_in(2)
+    grads(5)
+    dy_in(7)
+    grads(7)
+    gob[...] = go[...].astype(BF)
+    for q in range(1, XS):
+        go_copy(q).start()
 
     def combine(i):
         group(three(oret, i, CAP), o_r.at[i]).wait_recv()
@@ -370,31 +398,24 @@
 
     combine(7)
     returns(4)
-    grads(6)
-    grads(5)
+    grad_in(0)
+    grad_in(1)
     combine(6)
-    dy_in(7)
-    grads(7)
-    gob[...] = go[...].astype(BF)
-    for q in range(1, XS):
-        go_copy(q).start()
     returns(3)
+    grad_in(2)
+    grad_in(3)
+    grad_in(4)
+    sum_a()
     combine(5)
     returns(2)
-    grad_in(4)
-    grad_in(3)
-    grad_in(6)
-    grad_in(5)
-    grad_in(7)
-    sum_a()
+    sum_b()
     combine(4)
     returns(1)
     combine(3)
     returns(0)
-    sum_b()
     combine(2)
+    sum_c()
     combine(1)
-    sum_c()
     combine(0)
     group(dpf.at[pl.ds(1, 2 * YS - 1)], dc_r).wait_recv()
     for j in range(2 * YS):
@@ -450,8 +471,8 @@
             V((hidden, width), BF), V((hidden, width), BF), V((hidden, width), BF), V((depth, hidden), BF),
             V((8, ROWS, width), BF), V((8, ROWS, width), BF), V((8, ROWS, hidden), BF),
             V((8, ROWS, width), BF), V((8, ROWS, width), BF),
-            V((8, XS * depth, 128), BF), V((8, XS * depth, 128), BF),
-            V((8, XS * depth, 128), BF), V((8, XS * depth, 128), BF),
+            V((5, XS * depth, 128), BF), V((5, XS * depth, 128), BF),
+            V((4, XS * depth, 128), BF), V((4, XS * depth, 128), BF),
             V((8, toks, width), BF), V((8, toks, width), BF),
             V((depth, 768), F32), V((XS * depth, width), F32), V((XS * depth, width), BF), V((XS * depth, width), BF),
             V((8, 2 * depth, 128), F32), V((8, 2 * depth, 128), F32),

time: 99.7 us -> 95.3 us (0.956); the launches traced: 97.9 us -> 95.2 us
  Pallas kernels: 97.2 us -> 94.5 us
    pallas_call x1, Pallas kernels: 95.5 us -> 92.8 us  [shards(): pl.pallas_call(kernel, name='moe', out_shape=(jax.ShapeDtypeStruct((toks,...]
where the time goes in v4:
time: 95.3 us; the launch traced here: 95.2 us
  Pallas kernels  94.5 us (99%)
    pallas_call x1, Pallas kernels, shards(): pl.pallas_call(kernel, name='moe', out_shape=(jax.ShapeDtypeStruct((toks,...  92.8 us

profile of v4, /device:TPU:1, one launch (start us, length us, event | category | flops | bytes accessed | tf_op | source)
XLA Modules:
  0.0 95.2 jit_solution(3100806948103318297)
XLA Ops:
  0.6 92.8 %moe.1 = (bf16[128,1024]{1,0:T(8,128)(2,1)}, bf16[16,704]{1,0:T(8,128)(2,1)}, bf16[16,1024]{1,0:T(8,128)(2,1)}) custom-call(s32[6,128]{1,0:T(8,128)} %bitcast.6, f32[6,128]{1,0:T(8,128)} %bitcast.7, bf16[128,1024]{1,0:T(8,128)(2,1)} %tok_hbm.1, bf16[128,1024]{1,0:T(8,128)(2,1)} %dy_hbm.1, bf16[1,704,1024]{2,1,0:T(8,128)(2,1)} %bitcast.4, ...), custom_call_target="tpu_custom_call" | custom-call | tf_op jit(solution)/shard_map/moe/pallas_call | solution.py:457
  93.5 1.7 %settle.1 = (bf16[128,1024]{1,0:T(8,128)(2,1)}, bf16[1,16,704]{2,1,0:T(8,128)(2,1)}, bf16[1,16,1024]{2,1,0:T(8,128)(2,1)}) custom-call(bf16[128,1024]{1,0:T(8,128)(2,1)} %get-tuple-element.6.a_ref, bf16[16,704]{1,0:T(8,128)(2,1)} %get-tuple-element.7.b_ref, bf16[16,1024]{1,0:T(8,128)(2,1)} %get-tuple-element.8.c_ref), custom_call_target="tpu_custom_call" | custom-call | tf_op jit(solution)/shard_map/settle/pallas_call | solution.py:489

commit v5 on v4

--- a/solution.py
+++ b/solution.py
@@ -39,6 +39,7 @@
     choices = ids_hbm.shape[0]
     toks = tok_hbm.shape[0]
     half = toks // 2
+    lead = toks // 4 * 3
     d = lax.axis_index("dp")
     e = lax.axis_index("expert")
     core = lax.rem(d, 2)
@@ -78,9 +79,11 @@
         return way * (2 * lax.rem(i, 2) - 1)
 
     def tok_copy(i, h):
-        src = jnp.maximum(i - 2, 0)
+        src = max(i - 2, 0)
         rows = pl.ds(h * half, half)
-        return remote(tbuf.at[src, rows], tbuf.at[i, rows], t_s.at[jnp.minimum(i, 2) - 1], t_r.at[i, h],
+        if i == 1:
+            rows = pl.ds(h * lead, toks - lead if h else lead)
+        return remote(tbuf.at[src, rows], tbuf.at[i, rows], t_s.at[h if i == 1 else 2], t_r.at[i, h],
                       at(x, ring(out_step(i))))
 
     def dy_copy(i):
@@ -290,7 +293,7 @@
             o_copy(i, q).start()
 
     compact(0)
-    group(tbuf.at[0], t_s.at[0]).wait_send()
+    group(tbuf.at[0, pl.ds(0, lead)], t_s.at[0]).wait_send()
     m_copy(2).start()
     for h in (0, 1):
         tok_copy(2, h).start()
@@ -338,6 +341,7 @@
     gob[...] = go[...].astype(BF)
     for q in range(1, XS):
         go_copy(q).start()
+    returns(4)
 
     def combine(i):
         group(three(oret, i, CAP), o_r.at[i]).wait_recv()
@@ -397,7 +401,6 @@
             dc_copy(r).start()
 
     combine(7)
-    returns(4)
     grad_in(0)
     grad_in(1)
     combine(6)
@@ -426,7 +429,8 @@
             gin_ref[:, j * 128:j * 128 + width] = piece[depth:2 * depth, 0:width]
 
     seven = pl.ds(1, 7)
-    group(tbuf.at[pl.ds(2, 6)], t_s.at[1]).wait_send()
+    group(tbuf.at[0, pl.ds(lead, toks - lead)], t_s.at[1]).wait_send()
+    group(tbuf.at[pl.ds(2, 6)], t_s.at[2]).wait_send()
     group(idg.at[seven], m_s).wait_send()
     group(dbuf.at[seven], d_s).wait_send()
     group(rss.at[seven], r_s).wait_send()
@@ -450,7 +454,7 @@
 def shards(tokens, ids, gates, dy, wg, wu, wd, ad, au):
     toks, width = tokens.shape
     depth, hidden = ad.shape[1], ad.shape[2]
-    anyspace = pl.BlockSpec(memory_space=pl.ANY)
+    hbm = pl.BlockSpec(memory_space=pltpu.HBM)
     vmem = pl.BlockSpec(memory_space=pltpu.VMEM)
     dma = pltpu.SemaphoreType.DMA
     V = pltpu.VMEM
@@ -462,7 +466,7 @@
             jax.ShapeDtypeStruct((depth, hidden), BF),
             jax.ShapeDtypeStruct((depth, width), BF),
         ),
-        in_specs=[anyspace] * 9,
+        in_specs=[hbm] * 9,
         out_specs=(vmem, vmem, vmem),
         scratch_shapes=[
             V((8, toks, width), BF), V((8, toks, width), BF), V(ids.shape[::-1], ids.dtype), V((8, 16, toks), F32),
@@ -478,14 +482,15 @@
             V((8, 2 * depth, 128), F32), V((8, 2 * depth, 128), F32),
             V((2 * depth, 128), F32), V((2 * depth, 128), F32), V((2 * depth, 128), BF),
             V((8, 2 * depth, 128), BF),
-            dma((9,)), dma((2,)), dma((8, 2)), dma(()), dma((8,)), dma(()), dma((8,)), dma(()), dma(()),
+            dma((9,)), dma((3,)), dma((8, 2)), dma(()), dma((8,)), dma(()), dma((8,)), dma(()), dma(()),
             dma(()), dma((8,)), dma(()), dma((8,)), dma(()), dma((8,)), dma(()), dma((8,)),
             dma(()), dma((8, 2)), dma(()), dma(()), dma(()), dma(()), dma(()), dma(()), dma(()), dma(()),
             pltpu.SemaphoreType.REGULAR,
         ],
         compiler_params=pltpu.CompilerParams(
-            collective_id=0, has_side_effects=True, vmem_limit_bytes=61 * 1024 * 1024),
-    )(ids.T, gates.T, tokens, dy, wg.swapaxes(1, 2), wu.swapaxes(1, 2), wd, ad, au)
+            collective_id=0, has_side_effects=True, vmem_limit_bytes=48 * 1024 * 1024),
+    )(*(pltpu.with_memory_space_constraint(v, pltpu.HBM) for v in (
+        ids.T, gates.T, tokens, dy, wg.swapaxes(1, 2), wu.swapaxes(1, 2), wd, ad, au)))
     mixed, gin, gout = pl.pallas_call(
         settle,
         name="settle",
@@ -496,6 +501,7 @@
         ),
         in_specs=[vmem] * 3,
         out_specs=(vmem, vmem, vmem),
+        compiler_params=pltpu.CompilerParams(vmem_limit_bytes=4 * 1024 * 1024),
     )(mixed, gin, gout)
     return mixed, gin, gout
 

time: 95.3 us -> 93.8 us (0.984)
  Pallas kernels: 94.5 us -> 93 us
    pallas_call x1, Pallas kernels: 1.7 us -> 0.74 us  [shards(): pl.pallas_call(settle, name='settle', out_shape=(jax.ShapeDtypeStruct((to...]
where the time goes in v5:
time: 93.8 us; the launch traced here: 93.7 us
  Pallas kernels  93 us (99%)
    pallas_call x1, Pallas kernels, shards(): pl.pallas_call(kernel, name='moe', out_shape=(jax.ShapeDtypeStruct((toks,...  92.3 us

profile of v5, /device:TPU:1, one launch (start us, length us, event | category | flops | bytes accessed | tf_op | source)
XLA Modules:
  0.0 93.7 jit_solution(8038130667238609389)
XLA Ops:
  0.6 92.3 %moe.1 = (bf16[128,1024]{1,0:T(8,128)(2,1)S(1)}, bf16[16,704]{1,0:T(8,128)(2,1)S(1)}, bf16[16,1024]{1,0:T(8,128)(2,1)S(1)}) custom-call(s32[6,128]{1,0:T(8,128)} %bitcast.6, f32[6,128]{1,0:T(8,128)} %bitcast.7, bf16[128,1024]{1,0:T(8,128)(2,1)} %tok_hbm.1, bf16[128,1024]{1,0:T(8,128)(2,1)} %dy_hbm.1, bf16[1,704,1024]{2,1,0:T(8,128)(2,1)} %bitcast.4, ...), custom_call_target="tpu_custom_call" | custom-call | tf_op jit(solution)/shard_map/moe/pallas_call | solution.py:461
  92.9 0.7 settle.1

commit v6 on v5

--- a/solution.py
+++ b/solution.py
@@ -30,9 +30,9 @@
     mixed_ref, gin_ref, gout_ref,
     tbuf, dbuf, own, idg, mbuf, abuf, wg, wu, wd, ad,
     ssend, srecv, hbuf, osend, oret, lgs, lgr, lrs, lrr, rss, rsr,
-    gi, go, gob, gor, dpa, dpr, dpb, dpq, dpo, dpf,
+    gi, go, goc, goy, gox, gor, dpa, dpr, dpb, dpq, dpo, dpf,
     ld_sem, t_s, t_r, m_s, m_r, d_s, d_r, a_s, a_r, x_s, x_r, lg_s, lg_r,
-    o_s, o_r, lr_s, lr_r, r_s, r_r, go_s, go_r, da_s, da_r, db_s, db_r, dc_s, dc_r, far,
+    o_s, o_r, lr_s, lr_r, r_s, r_r, go_s, go_r, gy_s, gy_r, da_s, da_r, db_s, db_r, dc_s, dc_r, far,
 ):
     depth = ad_hbm.shape[1]
     hidden = wg_hbm.shape[1]
@@ -121,8 +121,12 @@
                       at(x, ring(-out_step(i))))
 
     def go_copy(q):
-        return remote(gob.at[pl.ds(q * depth, depth)], gor.at[pl.ds(q * depth, depth)],
+        return remote(gox.at[pl.ds(q * depth, depth)], gor.at[pl.ds(q * depth, depth)],
                       go_s, go_r, at(xq(q), z))
+
+    def gy_copy(r):
+        kk, dev = peer(r)
+        return remote(goc.at[kk], goy.at[r], gy_s, gy_r, dev)
 
     def da_copy(r):
         kk, dev = peer(r)
@@ -165,12 +169,6 @@
     loads[8].wait()
     idg[0, 8:8 + choices] = own[...].astype(F32)
     loads[0].wait()
-    pl.semaphore_wait(barrier, len(friends))
-
-    m_copy(1).start()
-    for h in (0, 1):
-        tok_copy(1, h).start()
-
     row_id = lax.broadcasted_iota(jnp.int32, (CAP, toks), 0).astype(F32)
     row_all = lax.broadcasted_iota(jnp.int32, (toks, toks), 0).astype(F32)
     lane_id = lax.broadcasted_iota(jnp.int32, (toks, ROWS), 1).astype(F32)
@@ -186,13 +184,17 @@
         mbuf[i] = m
         return m
 
-    def compact(i):
+    def picks(i):
         m = route(i)
-        hot = jnp.concatenate(
+        return jnp.concatenate(
             [(row_id == m[XS + q:XS + q + 1]).astype(F32) for q in range(XS)], axis=0).astype(BF)
+
+    def compact(i, hot):
         rows = mm(hot, tbuf[i]).astype(BF)
         srecv[i, 0:CAP] = rows[0:CAP]
         ssend[i, CAP:ROWS] = rows[CAP:ROWS]
+
+    def spread(i):
         for q in range(1, XS):
             x_copy(i, q).start()
 
@@ -279,11 +281,13 @@
 
     def tokens_in(i):
         m_copy(i).wait_recv()
+        hot = picks(i)
         for h in (0, 1):
             tok_copy(i, h).wait_recv()
             if 1 < i <= 5:
                 pass_on(i + 2, h)
-        compact(i)
+        compact(i, hot)
+        spread(i)
         if i == 1:
             pass_on(3, 0)
             pass_on(3, 1)
@@ -292,7 +296,13 @@
         for q in range(1, XS):
             o_copy(i, q).start()
 
-    compact(0)
+    compact(0, picks(0))
+    pl.semaphore_wait(barrier, len(friends))
+
+    m_copy(1).start()
+    for h in (0, 1):
+        tok_copy(1, h).start()
+    spread(0)
     group(tbuf.at[0, pl.ds(0, lead)], t_s.at[0]).wait_send()
     m_copy(2).start()
     for h in (0, 1):
@@ -338,19 +348,20 @@
     grads(5)
     dy_in(7)
     grads(7)
-    gob[...] = go[...].astype(BF)
-    for q in range(1, XS):
-        go_copy(q).start()
+    for j in range(2 * YS):
+        goc[j] = go[:, j * 128:(j + 1) * 128]
+    for r in range(1, 2 * YS):
+        gy_copy(r).start()
     returns(4)
 
     def combine(i):
-        group(three(oret, i, CAP), o_r.at[i]).wait_recv()
         mt = mbuf[i].T
         wt = jnp.zeros((toks, ROWS), F32)
         for q in range(XS):
             wt = jnp.where(lane_id == mt[:, XS + q:XS + q + 1] + float(q * CAP), mt[:, q:q + 1], wt)
         hi = wt.astype(BF)
         lo = (wt - hi.astype(F32)).astype(BF)
+        group(three(oret, i, CAP), o_r.at[i]).wait_recv()
         rows = oret[i]
         for h in (0, 1):
             keep = slice(h * half, (h + 1) * half)
@@ -369,26 +380,34 @@
             rs_copy(i, h).start()
 
     def sum_a():
-        group(gor.at[pl.ds(depth, 3 * depth)], go_r).wait_recv()
-        total = go[0:depth]
-        for q in range(1, XS):
-            total += gor[q * depth:(q + 1) * depth].astype(F32)
         for j in range(2 * YS):
-            cols = slice(j * 128, (j + 1) * 128)
-            dpa[j, 0:depth] = total[:, cols]
             if j * 128 < hidden:
-                dpa[j, depth:2 * depth] = gi[:, cols]
+                dpa[j] = gi[:, j * 128:(j + 1) * 128]
             else:
-                dpa[j, depth:2 * depth] = jnp.zeros((depth, 128), F32)
+                dpa[j] = jnp.zeros((depth, 128), F32)
         for r in range(1, 2 * YS):
             da_copy(r).start()
 
+    def sum_x():
+        group(goy.at[pl.ds(1, 2 * YS - 1)], gy_r).wait_recv()
+        mine = goc[k]
+        for r in range(1, 2 * YS):
+            mine += goy[r]
+        gox[...] = mine
+        for q in range(1, XS):
+            go_copy(q).start()
+
     def sum_b():
+        group(dpr.at[pl.ds(1, 2 * YS - 1)], da_r).wait_recv()
         mine = dpa[k]
-        group(dpr.at[pl.ds(1, 2 * YS - 1)], da_r).wait_recv()
         for r in range(1, 2 * YS):
             mine += dpr[r]
-        dpb[...] = mine
+        dpb[depth:2 * depth] = mine
+        group(gor.at[pl.ds(depth, 3 * depth)], go_r).wait_recv()
+        mine = gox[0:depth]
+        for q in range(1, XS):
+            mine += gor[q * depth:(q + 1) * depth]
+        dpb[0:depth] = mine
         pl.semaphore_wait(far, 1)
         db_copy().start()
 
@@ -409,6 +428,7 @@
     grad_in(3)
     grad_in(4)
     sum_a()
+    sum_x()
     combine(5)
     returns(2)
     sum_b()
@@ -435,7 +455,8 @@
     group(dbuf.at[seven], d_s).wait_send()
     group(rss.at[seven], r_s).wait_send()
     group(abuf.at[pl.ds(depth, 3 * depth)], a_s).wait_send()
-    group(gob.at[pl.ds(depth, 3 * depth)], go_s).wait_send()
+    group(gox.at[pl.ds(depth, 3 * depth)], go_s).wait_send()
+    group(goy.at[seven], gy_s).wait_send()
     group(ssend.at[:, pl.ds(CAP, 3 * CAP)], x_s).wait_send()
     group(osend.at[:, pl.ds(CAP, 3 * CAP)], o_s).wait_send()
     group(lgs.at[:, pl.ds(depth, 3 * depth)], lg_s).wait_send()
@@ -478,13 +499,14 @@
             V((5, XS * depth, 128), BF), V((5, XS * depth, 128), BF),
             V((4, XS * depth, 128), BF), V((4, XS * depth, 128), BF),
             V((8, toks, width), BF), V((8, toks, width), BF),
-            V((depth, 768), F32), V((XS * depth, width), F32), V((XS * depth, width), BF), V((XS * depth, width), BF),
-            V((8, 2 * depth, 128), F32), V((8, 2 * depth, 128), F32),
+            V((depth, 768), F32), V((XS * depth, width), F32), V((8, XS * depth, 128), F32), V((8, XS * depth, 128), F32),
+            V((XS * depth, 128), F32), V((XS * depth, 128), F32),
+            V((8, depth, 128), F32), V((8, depth, 128), F32),
             V((2 * depth, 128), F32), V((2 * depth, 128), F32), V((2 * depth, 128), BF),
             V((8, 2 * depth, 128), BF),
             dma((9,)), dma((3,)), dma((8, 2)), dma(()), dma((8,)), dma(()), dma((8,)), dma(()), dma(()),
             dma(()), dma((8,)), dma(()), dma((8,)), dma(()), dma((8,)), dma(()), dma((8,)),
-            dma(()), dma((8, 2)), dma(()), dma(()), dma(()), dma(()), dma(()), dma(()), dma(()), dma(()),
+            dma(()), dma((8, 2)), dma(()), dma(()), dma(()), dma(()), dma(()), dma(()), dma(()), dma(()), dma(()), dma(()),
             pltpu.SemaphoreType.REGULAR,
         ],
         compiler_params=pltpu.CompilerParams(

time: 93.8 us -> 95 us (1.013)
  Pallas kernels: 93 us -> 94.2 us
    pallas_call x1, Pallas kernels: 92.3 us -> 93.5 us  [shards(): pl.pallas_call(kernel, name='moe', out_shape=(jax.ShapeDtypeStruct((toks,...]
where the time goes in v6:
time: 95 us; the launch traced here: 94.9 us
  Pallas kernels  94.2 us (99%)
    pallas_call x1, Pallas kernels, shards(): pl.pallas_call(kernel, name='moe', out_shape=(jax.ShapeDtypeStruct((toks,...  93.5 us

profile of v6, /device:TPU:1, one launch (start us, length us, event | category | flops | bytes accessed | tf_op | source)
XLA Modules:
  0.0 94.9 jit_solution(6966280359064728127)
XLA Ops:
  0.6 93.5 %moe.1 = (bf16[128,1024]{1,0:T(8,128)(2,1)S(1)}, bf16[16,704]{1,0:T(8,128)(2,1)S(1)}, bf16[16,1024]{1,0:T(8,128)(2,1)S(1)}) custom-call(s32[6,128]{1,0:T(8,128)} %bitcast.6, f32[6,128]{1,0:T(8,128)} %bitcast.7, bf16[128,1024]{1,0:T(8,128)(2,1)} %tok_hbm.1, bf16[128,1024]{1,0:T(8,128)(2,1)} %dy_hbm.1, bf16[1,704,1024]{2,1,0:T(8,128)(2,1)} %bitcast.4, ...), custom_call_target="tpu_custom_call" | custom-call | tf_op jit(solution)/shard_map/moe/pallas_call | solution.py:482
  94.1 0.7 settle.1

commit v7 on v5

--- a/solution.py
+++ b/solution.py
@@ -165,12 +165,6 @@
     loads[8].wait()
     idg[0, 8:8 + choices] = own[...].astype(F32)
     loads[0].wait()
-    pl.semaphore_wait(barrier, len(friends))
-
-    m_copy(1).start()
-    for h in (0, 1):
-        tok_copy(1, h).start()
-
     row_id = lax.broadcasted_iota(jnp.int32, (CAP, toks), 0).astype(F32)
     row_all = lax.broadcasted_iota(jnp.int32, (toks, toks), 0).astype(F32)
     lane_id = lax.broadcasted_iota(jnp.int32, (toks, ROWS), 1).astype(F32)
@@ -186,13 +180,17 @@
         mbuf[i] = m
         return m
 
-    def compact(i):
+    def picks(i):
         m = route(i)
-        hot = jnp.concatenate(
+        return jnp.concatenate(
             [(row_id == m[XS + q:XS + q + 1]).astype(F32) for q in range(XS)], axis=0).astype(BF)
+
+    def compact(i, hot):
         rows = mm(hot, tbuf[i]).astype(BF)
         srecv[i, 0:CAP] = rows[0:CAP]
         ssend[i, CAP:ROWS] = rows[CAP:ROWS]
+
+    def spread(i):
         for q in range(1, XS):
             x_copy(i, q).start()
 
@@ -279,11 +277,13 @@
 
     def tokens_in(i):
         m_copy(i).wait_recv()
+        hot = picks(i)
         for h in (0, 1):
             tok_copy(i, h).wait_recv()
             if 1 < i <= 5:
                 pass_on(i + 2, h)
-        compact(i)
+        compact(i, hot)
+        spread(i)
         if i == 1:
             pass_on(3, 0)
             pass_on(3, 1)
@@ -292,7 +292,13 @@
         for q in range(1, XS):
             o_copy(i, q).start()
 
-    compact(0)
+    compact(0, picks(0))
+    pl.semaphore_wait(barrier, len(friends))
+
+    m_copy(1).start()
+    for h in (0, 1):
+        tok_copy(1, h).start()
+    spread(0)
     group(tbuf.at[0, pl.ds(0, lead)], t_s.at[0]).wait_send()
     m_copy(2).start()
     for h in (0, 1):
@@ -344,13 +350,13 @@
     returns(4)
 
     def combine(i):
-        group(three(oret, i, CAP), o_r.at[i]).wait_recv()
         mt = mbuf[i].T
         wt = jnp.zeros((toks, ROWS), F32)
         for q in range(XS):
             wt = jnp.where(lane_id == mt[:, XS + q:XS + q + 1] + float(q * CAP), mt[:, q:q + 1], wt)
         hi = wt.astype(BF)
         lo = (wt - hi.astype(F32)).astype(BF)
+        group(three(oret, i, CAP), o_r.at[i]).wait_recv()
         rows = oret[i]
         for h in (0, 1):
             keep = slice(h * half, (h + 1) * half)

time: 93.8 us -> 94 us (level)
  no operation moved by 1% of the time
where the time goes in v7:
time: 94 us; the launch traced here: 93.9 us
  Pallas kernels  93.3 us (99%)
    pallas_call x1, Pallas kernels, shards(): pl.pallas_call(kernel, name='moe', out_shape=(jax.ShapeDtypeStruct((toks,...  92.5 us

profile of v7, /device:TPU:1, one launch (start us, length us, event | category | flops | bytes accessed | tf_op | source)
XLA Modules:
  0.0 93.9 jit_solution(8172324312968074526)
XLA Ops:
  0.6 92.5 %moe.1 = (bf16[128,1024]{1,0:T(8,128)(2,1)S(1)}, bf16[16,704]{1,0:T(8,128)(2,1)S(1)}, bf16[16,1024]{1,0:T(8,128)(2,1)S(1)}) custom-call(s32[6,128]{1,0:T(8,128)} %bitcast.6, f32[6,128]{1,0:T(8,128)} %bitcast.7, bf16[128,1024]{1,0:T(8,128)(2,1)} %tok_hbm.1, bf16[128,1024]{1,0:T(8,128)(2,1)} %dy_hbm.1, bf16[1,704,1024]{2,1,0:T(8,128)(2,1)} %bitcast.4, ...), custom_call_target="tpu_custom_call" | custom-call | tf_op jit(solution)/shard_map/moe/pallas_call | solution.py:467
  93.2 0.7 settle.1
